TPU v7x, 32 devices: a whole 2x2x4 slice. The times are simulated.
32 devices in a mesh: seq: 8 (over z, y), dp: 4 (over x, core).
Axes of the slice: x: 2, y: 2, z: 4, core: 2. Of those that a mesh axis runs over, the one named last changes fastest.
Arguments:
- queries: bfloat16 [8192, 2048], P(('dp', 'seq')), parts along dimension 0, may hold values from -5 to 5
- keys: bfloat16 [8192, 128], P(('dp', 'seq')), parts along dimension 0, may hold values from -5 to 5
- values: bfloat16 [8192, 128], P(('dp', 'seq')), parts along dimension 0, may hold values from -5 to 5
- lengths: int32 [32], P('dp'), parts along dimension 0, may hold values from 1 to 1024, 2048 in all
- grad_out: bfloat16 [8192, 2048], P(('dp', 'seq')), parts along dimension 0, may hold values from -5 to 5
Outputs:
- attended: bfloat16 [8192, 2048], P(('dp', 'seq')), parts along dimension 0
- grad_queries: bfloat16 [8192, 2048], P(('dp', 'seq')), parts along dimension 0
- grad_keys: bfloat16 [8192, 128], P(('dp', 'seq')), parts along dimension 0
- grad_values: bfloat16 [8192, 128], P(('dp', 'seq')), parts along dimension 0
There are 4 independent parts, one for each index of `dp`. A program takes and returns all parts, laid end to end along the dimension named above; each array names one. Nothing has to cross between parts.
Inputs may be any that keep to these rules, and one draw needn't show every extreme that they name: The lengths sum to 2048.
All inputs are finite; a program needn't handle non-finite values.
Results may differ from a plain program's by a relative error of at most 0.018.
Values may be sent and summed in bfloat16 or wider, within the bound.
No kernel may reach another device: no remote copies, remote signals or barrier semaphores. Data moves between devices by JAX's collectives and lax.ppermute only.
A program may use at most 256 MiB of HBM per device.

v0:
```python
import functools
import math

import jax
import jax.numpy as jnp
from jax import lax
from jax.experimental import pallas as pl
from jax.experimental.pallas import tpu as pltpu
from jax.sharding import PartitionSpec as P

NEG_FILL = -1e30
LOG2_E = 1.4426950408889634


def passed_along(value, axis, steps):
    count = lax.axis_size(axis)
    first, last = (max(0, -steps), min(count, count - steps))
    return lax.ppermute(value, axis, [(source, source + steps) for source in range(first, last)])


def dot_nt(left, right):
    return lax.dot_general(left, right, (((1,), (1,)), ((), ())), preferred_element_type=jnp.float32)


def dot_nn(left, right):
    return lax.dot_general(left, right, (((1,), (0,)), ((), ())), preferred_element_type=jnp.float32)


def attention_kernel(
    slot_count,
    head_count,
    score_scale,
    start_ref,
    q_ref,
    qt_ref,
    g_ref,
    gt_ref,
    kv_ref,
    out_ref,
    dq_ref,
    grad_ref,
    bias_ref,
    vext_ref,
):
    tokens = q_ref.shape[0]
    width = kv_ref.shape[2] // 2
    factor = score_scale * LOG2_E
    row_start = start_ref[...]
    for slot in range(slot_count):
        key_pos = lax.broadcasted_iota(jnp.int32, (tokens, tokens), 1) - slot * tokens
        visible = key_pos >= row_start
        if slot == 0:
            visible = visible & (key_pos <= lax.broadcasted_iota(jnp.int32, (tokens, tokens), 0))
        bias_ref[slot] = jnp.where(visible, 0.0, NEG_FILL)
        vext_ref[slot, :, :width] = kv_ref[slot, :, width:]
        vext_ref[slot, :, width:] = jnp.ones((tokens, width), jnp.bfloat16)
        grad_ref[slot] = jnp.zeros((2 * width, tokens), jnp.float32)

    def one_head(head, carry):
        lanes = pl.ds(pl.multiple_of(head * width, width), width)
        q = q_ref[:, lanes]
        g = g_ref[:, lanes]
        qt = qt_ref[lanes, :]
        gt = gt_ref[lanes, :]
        scores = []
        top = None
        for slot in range(slot_count):
            s = dot_nt(q, kv_ref[slot, :, :width]) * factor + bias_ref[slot]
            scores.append(s)
            top = s if top is None else jnp.maximum(top, s)
        top = jnp.max(top, axis=1, keepdims=True)
        weights = []
        acc = None
        for slot in range(slot_count):
            w = jnp.exp2(scores[slot] - top).astype(jnp.bfloat16)
            weights.append(w)
            part = dot_nn(w, vext_ref[slot])
            acc = part if acc is None else acc + part
        inverse = 1.0 / acc[:, width:]
        out = (acc[:, :width] * inverse).astype(jnp.bfloat16)
        out_ref[:, lanes] = out
        delta = jnp.sum(g.astype(jnp.float32) * out.astype(jnp.float32), axis=1, keepdims=True)
        inverse = jnp.concatenate([inverse] * (tokens // width), axis=1)
        dq = None
        for slot in range(slot_count):
            dp = dot_nt(g, kv_ref[slot, :, width:])
            w = weights[slot].astype(jnp.float32) * inverse
            ds = (w * (dp - delta)).astype(jnp.bfloat16)
            part = dot_nn(ds, kv_ref[slot, :, :width])
            dq = part if dq is None else dq + part
            grad_ref[slot, :width] += dot_nn(qt, ds)
            grad_ref[slot, width:] += dot_nn(gt, w.astype(jnp.bfloat16))
        dq_ref[:, lanes] = (score_scale * dq).astype(jnp.bfloat16)
        return carry

    lax.fori_loop(0, head_count, one_head, 0)


def local_math(start, q, qt, g, gt, kv, head_count, score_scale):
    slot_count, tokens, both = kv.shape
    vmem = pl.BlockSpec(memory_space=pltpu.VMEM)
    return pl.pallas_call(
        functools.partial(attention_kernel, slot_count, head_count, score_scale),
        out_shape=(
            jax.ShapeDtypeStruct(q.shape, jnp.bfloat16),
            jax.ShapeDtypeStruct(q.shape, jnp.bfloat16),
            jax.ShapeDtypeStruct((slot_count, both, tokens), jnp.float32),
        ),
        in_specs=[vmem] * 6,
        out_specs=(vmem, vmem, vmem),
        scratch_shapes=[
            pltpu.VMEM((slot_count, tokens, tokens), jnp.float32),
            pltpu.VMEM((slot_count, tokens, both), jnp.bfloat16),
        ],
        compiler_params=pltpu.CompilerParams(vmem_limit_bytes=40 << 20),
        name="attention",
    )(start, q, qt, g, gt, kv)


def shards(queries, keys, values, lengths, grad_out):
    tokens = queries.shape[0]
    width = keys.shape[1]
    head_count = queries.shape[1] // width
    axis_size = lax.axis_size("seq")
    reach = min(8, axis_size // 2)
    rank = lax.axis_index("seq")
    score_scale = 1.0 / math.sqrt(width)

    own = jnp.concatenate([keys, values], axis=1)
    far = [passed_along(own, "seq", 1)]
    if reach > 1:
        far.append(passed_along(own, "seq", 2))
    window = jnp.stack(far)
    while window.shape[0] < reach:
        window = jnp.concatenate([window, passed_along(window, "seq", window.shape[0])], axis=0)
    window = jnp.concatenate([own[None], window], axis=0)

    first = rank * tokens
    positions = first + jnp.arange(tokens, dtype=jnp.int32)
    doc_ends = jnp.cumsum(lengths)
    starts = jnp.max(jnp.where(doc_ends[None, :] <= positions[:, None], doc_ends[None, :], 0), axis=1)
    starts = (starts - first).astype(jnp.int32)[:, None]

    out, dq, grads = local_math(
        starts, queries, queries.T, grad_out, grad_out.T, window, head_count, score_scale
    )
    total = grads[0]
    rest = grads[1:]
    while rest.shape[0] > 2:
        half = rest.shape[0] // 2
        moved = passed_along(rest[half:].astype(jnp.bfloat16), "seq", -half)
        rest = rest[:half] + moved.astype(jnp.float32)
    for offset in range(rest.shape[0]):
        moved = passed_along(rest[offset].astype(jnp.bfloat16), "seq", -1 - offset)
        total = total + moved.astype(jnp.float32)
    grad_keys = (score_scale * total[:width]).astype(jnp.bfloat16).T
    grad_values = total[width:].astype(jnp.bfloat16).T
    return (out, dq, grad_keys, grad_values)


def solution(mesh):
    rows = P(("dp", "seq"), None)
    return jax.shard_map(
        shards,
        mesh=mesh,
        in_specs=(rows, rows, rows, P("dp"), rows),
        out_specs=(rows, rows, rows, rows),
        check_vma=False,
    )
```

profile of v0, /device:TPU:0, one launch (start us, length us, event | category | flops | bytes accessed | tf_op | source)
XLA Modules:
  0.0 79.3 jit_solution(5189710956824825879)
XLA Ops:
  0.6 0.9 %constant_dynamic-update-slice_fusion.1 = bf16[256,256]{1,0:T(8,128)(2,1)S(1)} fusion(bf16[256,128]{1,0:T(8,128)(2,1)} %param.6), kind=kLoop, calls=%fused_computation.15 | loop fusion | bytes 131072
  1.5 0.9 %constant_dynamic-update-slice_fusion = bf16[256,256]{1,0:T(8,128)(2,1)S(1)} fusion(bf16[256,256]{1,0:T(8,128)(2,1)S(1)} %constant_dynamic-update-slice_fusion.1, bf16[256,128]{1,0:T(8,128)(2,1)} %param.7), kind=kLoop, calls=%fused_computation.14 | loop fusion | bytes 131072 | tf_op jit(solution)/shard_map/concatenate | solution.py:129
  2.4 5.0 %collective-permute-start.1 = (bf16[256,256]{1,0:T(8,128)(2,1)S(1)}, bf16[256,256]{1,0:T(8,128)(2,1)S(1)}, u32[]{:S(2)}, u32[]{:S(2)}) collective-permute-start(bf16[256,256]{1,0:T(8,128)(2,1)S(1)} %constant_dynamic-update-slice_fusion), channel_id=1, source_target_pairs={{0,8},{4,12},{8,16},{12,20},{16,24},{20,28},{1,9},{5,13},{9,17},{1... | collective-permute-start | bytes 393224 | tf_op jit(solution)/shard_map/ppermute | solution.py:18
  7.3 3.4 %collective-permute-start = (bf16[256,256]{1,0:T(8,128)(2,1)S(1)}, bf16[256,256]{1,0:T(8,128)(2,1)S(1)}, u32[]{:S(2)}, u32[]{:S(2)}) collective-permute-start(bf16[256,256]{1,0:T(8,128)(2,1)S(1)} %constant_dynamic-update-slice_fusion), channel_id=1, source_target_pairs={{0,4},{4,8},{8,12},{12,16},{16,20},{20,24},{24,28},{1,5},{5,9},{9,... | collective-permute-start | bytes 393224 | tf_op jit(solution)/shard_map/ppermute | solution.py:18
  10.8 0.8 %reduce-window.8 = s32[8,1]{0,1:T(1,128)S(1)} reduce-window(s32[8,1]{0,1:T(1,128)} %bitcast.29, s32[]{:T(128)} %constant.6.clone.1), window={size=8x1 pad=7_0x0_0}, to_apply=%region_0.0 | reduce-window | flops 56 | bytes 68 | tf_op jit(solution)/shard_map/reduce-window.3
  11.6 1.7 %collective-permute-done = bf16[256,256]{1,0:T(8,128)(2,1)S(1)} collective-permute-done((bf16[256,256]{1,0:T(8,128)(2,1)S(1)}, bf16[256,256]{1,0:T(8,128)(2,1)S(1)}, u32[]{:S(2)}, u32[]{:S(2)}) %collective-permute-start) | collective-permute-done | bytes 131104 | tf_op jit(solution)/shard_map/ppermute | solution.py:18
  13.3 0.7 pad_maximum_fusion.1
  14.0 6.0 %collective-permute-start.2 = (bf16[2,256,256]{2,1,0:T(8,128)(2,1)}, bf16[2,256,256]{2,1,0:T(8,128)(2,1)}, u32[]{:S(2)}, u32[]{:S(2)}) collective-permute-start(bf16[2,256,256]{2,1,0:T(8,128)(2,1)} %pad_maximum_fusion.1), channel_id=1, source_target_pairs={{0,8},{4,12},{8,16},{12,20},{16,24},{20,28},{1,9},{5,13},{9,17},{1... | collective-permute-start | bytes 786440 | tf_op jit(solution)/shard_map/ppermute | solution.py:18
  20.0 0.1 select_reduce_fusion
  20.1 0.1 copy.20.start_ref
  20.2 1.5 %copy.18 = bf16[256,2048]{0,1:T(8,128)(2,1)S(1)} copy(bf16[256,2048]{1,0:T(8,128)(2,1)} %q_ref.1) | data formatting | bytes 2097152 | tf_op args[0]
  21.7 1.3 %copy.19 = bf16[256,2048]{0,1:T(8,128)(2,1)} copy(bf16[256,2048]{1,0:T(8,128)(2,1)S(1)} %copy-done.1) | data formatting | bytes 2097152 | tf_op args[4]
  23.1 0.7 collective-permute-done.2
  23.7 1.1 %pad_maximum_fusion.kv_ref = bf16[5,256,256]{2,1,0:T(8,128)(2,1)S(1)} fusion(bf16[2,256,256]{2,1,0:T(8,128)(2,1)} %collective-permute-done.2, bf16[1,256,256]{2,1,0:T(8,128)(2,1)S(1)} %bitcast.23, bf16[1,256,256]{2,1,0:T(8,128)(2,1)S(1)} %bitcast.25, bf16[1,256,256]{2,1,0:T(8,128)(2,1)} %bitcast.26), kind=kLoop, calls=%fused_computation | loop fusion | flops 983040 | bytes 1310720 | tf_op jit(solution)/shard_map/concatenate | solution.py:136
  24.8 35.2 %attention.1 = (bf16[256,2048]{1,0:T(8,128)(2,1)}, bf16[256,2048]{1,0:T(8,128)(2,1)}, f32[5,256,256]{2,1,0:T(8,128)S(1)}) custom-call(s32[256,1]{1,0:T(8,128)S(1)} %copy.20.start_ref, bf16[256,2048]{1,0:T(8,128)(2,1)S(1)} %copy-done, bf16[2048,256]{1,0:T(8,128)(2,1)S(1)} %bitcast.20, bf16[256,2048]{1,0:T(8,128)(2,1)S(1)} %copy-done.1, ...), custom_call_target="tpu_custom_call" | custom-call | tf_op jit(solution)/shard_map/attention/pallas_call | solution.py:102
  60.1 1.3 %collective-permute-start.3 = (bf16[2,256,256]{2,1,0:T(8,128)(2,1)S(1)}, bf16[2,256,256]{2,1,0:T(8,128)(2,1)S(1)}, u32[]{:S(2)}, u32[]{:S(2)}) collective-permute-start(bf16[2,256,256]{2,1,0:T(8,128)(2,1)S(1)} %slice.53), channel_id=1, source_target_pairs={{8,0},{12,4},{16,8},{20,12},{24,16},{28,20},{9,1},{13,5},{17,9},{2... | collective-permute-start | bytes 786440 | tf_op jit(solution)/shard_map/ppermute | solution.py:18
  61.4 7.4 %collective-permute-done.3 = bf16[2,256,256]{2,1,0:T(8,128)(2,1)S(1)} collective-permute-done((bf16[2,256,256]{2,1,0:T(8,128)(2,1)S(1)}, bf16[2,256,256]{2,1,0:T(8,128)(2,1)S(1)}, u32[]{:S(2)}, u32[]{:S(2)}) %collective-permute-start.3) | collective-permute-done | bytes 262176 | tf_op jit(solution)/shard_map/ppermute | solution.py:18
  68.8 0.1 add_convert_fusion
  68.9 1.3 %collective-permute-start.4 = (bf16[256,256]{1,0:T(8,128)(2,1)S(1)}, bf16[256,256]{1,0:T(8,128)(2,1)S(1)}, u32[]{:S(2)}, u32[]{:S(2)}) collective-permute-start(bf16[256,256]{1,0:T(8,128)(2,1)S(1)} %get-tuple-element.22), channel_id=1, source_target_pairs={{4,0},{8,4},{12,8},{16,12},{20,16},{24,20},{28,24},{5,1},{9,5},{13... | collective-permute-start | bytes 393224 | tf_op jit(solution)/shard_map/ppermute | solution.py:18
  70.2 1.3 %collective-permute-start.5 = (bf16[256,256]{1,0:T(8,128)(2,1)S(1)}, bf16[256,256]{1,0:T(8,128)(2,1)S(1)}, u32[]{:S(2)}, u32[]{:S(2)}) collective-permute-start(bf16[256,256]{1,0:T(8,128)(2,1)S(1)} %get-tuple-element.23), channel_id=1, source_target_pairs={{8,0},{12,4},{16,8},{20,12},{24,16},{28,20},{9,1},{13,5},{17,9},{2... | collective-permute-start | bytes 393224 | tf_op jit(solution)/shard_map/ppermute | solution.py:18
  71.5 4.3 %collective-permute-done.4 = bf16[256,256]{1,0:T(8,128)(2,1)S(1)} collective-permute-done((bf16[256,256]{1,0:T(8,128)(2,1)S(1)}, bf16[256,256]{1,0:T(8,128)(2,1)S(1)}, u32[]{:S(2)}, u32[]{:S(2)}) %collective-permute-start.4) | collective-permute-done | bytes 131104 | tf_op jit(solution)/shard_map/ppermute | solution.py:18
  75.8 2.0 %collective-permute-done.5 = bf16[256,256]{1,0:T(8,128)(2,1)S(1)} collective-permute-done((bf16[256,256]{1,0:T(8,128)(2,1)S(1)}, bf16[256,256]{1,0:T(8,128)(2,1)S(1)}, u32[]{:S(2)}, u32[]{:S(2)}) %collective-permute-start.5) | collective-permute-done | bytes 131104 | tf_op jit(solution)/shard_map/ppermute | solution.py:18
  77.8 0.7 copy.21
  78.6 0.7 copy.22
  (16 shorter events, 0.1 us)
Async XLA Ops:
  2.3 10.9 %copy-start.3 = (bf16[256,256]{1,0:T(8,128)(2,1)}, bf16[256,256]{1,0:T(8,128)(2,1)S(1)}, u32[]{:S(2)}) copy-start(bf16[256,256]{1,0:T(8,128)(2,1)S(1)} %constant_dynamic-update-slice_fusion) | copy-start | bytes 393220
  2.4 9.3 %collective-permute-start.1 = (bf16[256,256]{1,0:T(8,128)(2,1)S(1)}, bf16[256,256]{1,0:T(8,128)(2,1)S(1)}, u32[]{:S(2)}, u32[]{:S(2)}) collective-permute-start(bf16[256,256]{1,0:T(8,128)(2,1)S(1)} %constant_dynamic-update-slice_fusion), channel_id=1, source_target_pairs={{0,8},{4,12},{8,16},{12,20},{16,24},{20,28},{1,9},{5,13},{9,17},{1... | collective-permute-start | bytes 393224 | tf_op jit(solution)/shard_map/ppermute | solution.py:18
  7.3 5.9 %collective-permute-start = (bf16[256,256]{1,0:T(8,128)(2,1)S(1)}, bf16[256,256]{1,0:T(8,128)(2,1)S(1)}, u32[]{:S(2)}, u32[]{:S(2)}) collective-permute-start(bf16[256,256]{1,0:T(8,128)(2,1)S(1)} %constant_dynamic-update-slice_fusion), channel_id=1, source_target_pairs={{0,4},{4,8},{8,12},{12,16},{16,20},{20,24},{24,28},{1,5},{5,9},{9,... | collective-permute-start | bytes 393224 | tf_op jit(solution)/shard_map/ppermute | solution.py:18
  13.3 8.5 %copy-start.1 = (bf16[256,2048]{1,0:T(8,128)(2,1)S(1)}, bf16[256,2048]{1,0:T(8,128)(2,1)}, u32[]{:S(2)}) copy-start(bf16[256,2048]{1,0:T(8,128)(2,1)} %g_ref.1) | copy-start | bytes 3145732
  14.0 9.7 %collective-permute-start.2 = (bf16[2,256,256]{2,1,0:T(8,128)(2,1)}, bf16[2,256,256]{2,1,0:T(8,128)(2,1)}, u32[]{:S(2)}, u32[]{:S(2)}) collective-permute-start(bf16[2,256,256]{2,1,0:T(8,128)(2,1)} %pad_maximum_fusion.1), channel_id=1, source_target_pairs={{0,8},{4,12},{8,16},{12,20},{16,24},{20,28},{1,9},{5,13},{9,17},{1... | collective-permute-start | bytes 786440 | tf_op jit(solution)/shard_map/ppermute | solution.py:18
  21.7 3.1 %copy-start = (bf16[256,2048]{1,0:T(8,128)(2,1)S(1)}, bf16[256,2048]{1,0:T(8,128)(2,1)}, u32[]{:S(2)}) copy-start(bf16[256,2048]{1,0:T(8,128)(2,1)} %q_ref.1) | copy-start | bytes 3145732
  23.1 1.8 %copy-start.2 = (bf16[256,2048]{0,1:T(8,128)(2,1)S(1)}, bf16[256,2048]{0,1:T(8,128)(2,1)}, u32[]{:S(2)}) copy-start(bf16[256,2048]{0,1:T(8,128)(2,1)} %copy.19) | copy-start | bytes 3145732
  60.1 8.7 %collective-permute-start.3 = (bf16[2,256,256]{2,1,0:T(8,128)(2,1)S(1)}, bf16[2,256,256]{2,1,0:T(8,128)(2,1)S(1)}, u32[]{:S(2)}, u32[]{:S(2)}) collective-permute-start(bf16[2,256,256]{2,1,0:T(8,128)(2,1)S(1)} %slice.53), channel_id=1, source_target_pairs={{8,0},{12,4},{16,8},{20,12},{24,16},{28,20},{9,1},{13,5},{17,9},{2... | collective-permute-start | bytes 786440 | tf_op jit(solution)/shard_map/ppermute | solution.py:18
  68.9 6.9 %collective-permute-start.4 = (bf16[256,256]{1,0:T(8,128)(2,1)S(1)}, bf16[256,256]{1,0:T(8,128)(2,1)S(1)}, u32[]{:S(2)}, u32[]{:S(2)}) collective-permute-start(bf16[256,256]{1,0:T(8,128)(2,1)S(1)} %get-tuple-element.22), channel_id=1, source_target_pairs={{4,0},{8,4},{12,8},{16,12},{20,16},{24,20},{28,24},{5,1},{9,5},{13... | collective-permute-start | bytes 393224 | tf_op jit(solution)/shard_map/ppermute | solution.py:18
  70.2 7.5 %collective-permute-start.5 = (bf16[256,256]{1,0:T(8,128)(2,1)S(1)}, bf16[256,256]{1,0:T(8,128)(2,1)S(1)}, u32[]{:S(2)}, u32[]{:S(2)}) collective-permute-start(bf16[256,256]{1,0:T(8,128)(2,1)S(1)} %get-tuple-element.23), channel_id=1, source_target_pairs={{8,0},{12,4},{16,8},{20,12},{24,16},{28,20},{9,1},{13,5},{17,9},{2... | collective-permute-start | bytes 393224 | tf_op jit(solution)/shard_map/ppermute | solution.py:18
where the time goes:
time: 79.7 us; the launch traced here: 79.3 us
  Pallas kernels  35.2 us (44%)
  starting transfers between devices  18.3 us (23%)
  waiting for transfers between devices  16 us (20%)
  local copies, waits for them, and re-layouts  6.18 us (8%)
  other arithmetic  2.84 us (4%)
    pallas_call x1, Pallas kernels, local_math(): pl.pallas_call(functools.partial(attention_kernel, slot_count, head_count...  35.2 us
    ppermute x6, starting transfers between devices, passed_along(): lax.ppermute(value, axis, [(source, source + steps) for source in range(f...  18.3 us
    ppermute x6, waiting for transfers between devices, passed_along(): lax.ppermute(value, axis, [(source, source + steps) for source in range(f...  16 us
    unnamed x13, local copies, waits for them, and re-layouts  5.13 us
  transfers between devices with their start and end apart: 6, of which 5 were waited for; matrix products, arithmetic and copies ran while one was open for 5% of the time, Pallas kernels for 0%

commit v1 on v0

v1 whole, which is shorter than its diff:
```python
import functools
import math

import jax
import jax.numpy as jnp
from jax import lax
from jax.experimental import pallas as pl
from jax.experimental.pallas import tpu as pltpu
from jax.sharding import PartitionSpec as P

NEG_FILL = -1e30
LOG2_E = 1.4426950408889634


def ring_shift(value, steps):
    count = lax.axis_size("seq")
    return lax.ppermute(value, "seq", [(i, (i + steps) % count) for i in range(count)])


def dot_nt(left, right):
    return lax.dot_general(left, right, (((1,), (1,)), ((), ())), preferred_element_type=jnp.float32)


def dot_nn(left, right):
    return lax.dot_general(left, right, (((1,), (0,)), ((), ())), preferred_element_type=jnp.float32)


def head_lanes(head, width):
    return pl.ds(pl.multiple_of(head * width, width), width)


def take_rows(ref, group, pack, width):
    heads = [ref[:, head_lanes(group * pack + i, width)] for i in range(pack)]
    return jnp.concatenate(heads, axis=0)


def take_columns(ref, group, pack, width):
    heads = [ref[head_lanes(group * pack + i, width), :] for i in range(pack)]
    return jnp.concatenate(heads, axis=1)


def put_rows(ref, group, pack, width, value):
    tokens = value.shape[0] // pack
    for i in range(pack):
        ref[:, head_lanes(group * pack + i, width)] = value[i * tokens : (i + 1) * tokens]


def split_chain(lefts, rights, parts):
    step = lefts[0].shape[0] // parts
    sums = [None] * parts
    for left, right in zip(lefts, rights):
        for i in range(parts):
            part = dot_nn(left[i * step : (i + 1) * step], right)
            sums[i] = part if sums[i] is None else sums[i] + part
    return jnp.concatenate(sums, axis=0)


def row_dots(left, right):
    return jnp.sum(left.astype(jnp.float32) * right.astype(jnp.float32), axis=1, keepdims=True)


def backward_group(group, pack, width, g, delta, slots, q_t, g_t, weights, kv_refs, grad_ref):
    tokens = kv_refs[0].shape[0] // 2
    steps = []
    for index, (w, kv_ref) in enumerate(zip(weights, kv_refs)):
        dp = dot_nt(g, kv_ref[tokens:])
        ds = (w.astype(jnp.float32) * (dp - delta)).astype(jnp.bfloat16)
        steps.append(ds)
        grad_ref[index, :width] += dot_nn(q_t, ds)
        grad_ref[index, width:] += dot_nn(g_t, w)
    return split_chain(steps, [kv_ref[:tokens] for kv_ref in kv_refs], 2)


def first_kernel(slot_count, near, pack, head_count, score_scale, *refs):
    start_ref, q_ref, qt_ref, g_ref, gt_ref = refs[:5]
    kv_refs = refs[5 : 5 + slot_count]
    out_ref, dq_ref, grad_out_ref, kept_ref, bias_ref, vext_ref, grad_ref = refs[5 + slot_count :]
    tokens = q_ref.shape[0]
    width = q_ref.shape[1] // head_count
    rows = pack * tokens
    factor = score_scale * LOG2_E
    row_start = start_ref[...]
    for slot in range(slot_count):
        key_pos = lax.broadcasted_iota(jnp.int32, (tokens, tokens), 1) - slot * tokens
        visible = key_pos >= row_start
        if slot == 0:
            visible = visible & (key_pos <= lax.broadcasted_iota(jnp.int32, (tokens, tokens), 0))
        bias_ref[slot] = jnp.where(visible, 0.0, NEG_FILL)
        vext_ref[slot, :, :width] = kv_refs[slot][tokens:]
        vext_ref[slot, :, width:] = jnp.ones((tokens, width), jnp.bfloat16)
    grad_ref[...] = jnp.zeros(grad_ref.shape, jnp.float32)

    def one_group(group, carry):
        q = take_rows(q_ref, group, pack, width)
        g = take_rows(g_ref, group, pack, width)
        scores = []
        top = None
        for slot in range(slot_count):
            s = dot_nt(q, kv_refs[slot][:tokens]).reshape(pack, tokens, tokens)
            s = (s * factor + bias_ref[slot][None]).reshape(rows, tokens)
            scores.append(s)
            top = s if top is None else jnp.maximum(top, s)
        top = jnp.max(top, axis=1, keepdims=True)
        weights = [jnp.exp2(s - top).astype(jnp.bfloat16) for s in scores]
        total = split_chain(weights, [vext_ref[slot] for slot in range(slot_count)], 2)
        inverse = 1.0 / total[:, width:]
        out = (total[:, :width] * inverse).astype(jnp.bfloat16)
        put_rows(out_ref, group, pack, width, out)
        delta = row_dots(g, out)
        inverse = jnp.concatenate([inverse] * (tokens // width), axis=1)
        weights = [(w.astype(jnp.float32) * inverse).astype(jnp.bfloat16) for w in weights]
        group_rows = pl.ds(pl.multiple_of(group * rows, rows), rows)
        for slot in range(near):
            kept_ref[slot, group_rows] = weights[slot]
        q_t = take_columns(qt_ref, group, pack, width)
        g_t = take_columns(gt_ref, group, pack, width)
        dq = backward_group(
            group, pack, width, g, delta, slot_count, q_t, g_t, weights[near:], kv_refs[near:], grad_ref
        )
        put_rows(dq_ref, group, pack, width, dq)
        return carry

    lax.fori_loop(0, head_count // pack, one_group, 0)
    grad_out_ref[...] = grad_ref[...].astype(grad_out_ref.dtype)


def later_kernel(first_slot, slots, pack, head_count, dq_scale, *refs):
    qt_ref, g_ref, gt_ref, out_ref, kept_ref, dq_in_ref = refs[:6]
    kv_refs = refs[6 : 6 + slots]
    dq_ref, grad_ref = refs[6 + slots :]
    tokens = g_ref.shape[0]
    width = g_ref.shape[1] // head_count
    rows = pack * tokens
    grad_ref[...] = jnp.zeros(grad_ref.shape, jnp.float32)

    def one_group(group, carry):
        g = take_rows(g_ref, group, pack, width)
        delta = row_dots(g, take_rows(out_ref, group, pack, width))
        group_rows = pl.ds(pl.multiple_of(group * rows, rows), rows)
        weights = [kept_ref[first_slot + index, group_rows] for index in range(slots)]
        q_t = take_columns(qt_ref, group, pack, width)
        g_t = take_columns(gt_ref, group, pack, width)
        dq = backward_group(
            group, pack, width, g, delta, slots, q_t, g_t, weights, kv_refs, grad_ref
        )
        dq = dq + take_rows(dq_in_ref, group, pack, width)
        put_rows(dq_ref, group, pack, width, (dq * dq_scale).astype(dq_ref.dtype))
        return carry

    lax.fori_loop(0, head_count // pack, one_group, 0)


VMEM = pl.BlockSpec(memory_space=pltpu.VMEM)


def first_call(start, q, qt, g, gt, kvs, near, pack, head_count, score_scale):
    slot_count = len(kvs)
    tokens = q.shape[0]
    width = q.shape[1] // head_count
    far = slot_count - near
    return pl.pallas_call(
        functools.partial(first_kernel, slot_count, near, pack, head_count, score_scale),
        out_shape=(
            jax.ShapeDtypeStruct(q.shape, jnp.bfloat16),
            jax.ShapeDtypeStruct(q.shape, jnp.float32),
            jax.ShapeDtypeStruct((far, 2 * width, tokens), jnp.bfloat16),
            jax.ShapeDtypeStruct((near, head_count * tokens, tokens), jnp.bfloat16),
        ),
        in_specs=[VMEM] * (5 + slot_count),
        out_specs=(VMEM,) * 4,
        scratch_shapes=[
            pltpu.VMEM((slot_count, tokens, tokens), jnp.float32),
            pltpu.VMEM((slot_count, tokens, 2 * width), jnp.bfloat16),
            pltpu.VMEM((far, 2 * width, tokens), jnp.float32),
        ],
        compiler_params=pltpu.CompilerParams(vmem_limit_bytes=40 << 20),
        name="forward_far",
    )(start, q, qt, g, gt, *kvs)


def later_call(qt, g, gt, out, kept, dq, kvs, first_slot, pack, head_count, dq_scale, last):
    slots = len(kvs)
    tokens = g.shape[0]
    width = g.shape[1] // head_count
    return pl.pallas_call(
        functools.partial(later_kernel, first_slot, slots, pack, head_count, dq_scale),
        out_shape=(
            jax.ShapeDtypeStruct(g.shape, jnp.bfloat16 if last else jnp.float32),
            jax.ShapeDtypeStruct((slots, 2 * width, tokens), jnp.float32),
        ),
        in_specs=[VMEM] * (6 + slots),
        out_specs=(VMEM,) * 2,
        compiler_params=pltpu.CompilerParams(vmem_limit_bytes=24 << 20),
        name="backward_near",
    )(qt, g, gt, out, kept, dq, *kvs)


def shards(queries, keys, values, lengths, grad_out):
    tokens = queries.shape[0]
    width = keys.shape[1]
    head_count = queries.shape[1] // width
    reach = min(8, lax.axis_size("seq") // 2)
    rank = lax.axis_index("seq")
    score_scale = 1.0 / math.sqrt(width)
    pack = math.gcd(8, head_count)

    own = jnp.concatenate([keys, values], axis=0)
    window = [own]
    if reach > 1:
        two = ring_shift(own, 2)
        one = ring_shift(own, 1)
        window += [one, two]
    else:
        window += [ring_shift(own, 1)]
    if reach > 2:
        four = ring_shift(two, 2)
        three = ring_shift(two, 1)
        window += [three, four]
    while len(window) <= reach:
        shift = len(window) - 1
        window += [ring_shift(part, shift) for part in window[1:]]

    first = rank * tokens
    positions = first + jnp.arange(tokens, dtype=jnp.int32)
    doc_ends = jnp.cumsum(lengths)
    starts = jnp.max(jnp.where(doc_ends[None, :] <= positions[:, None], doc_ends[None, :], 0), axis=1)
    starts = (starts - first).astype(jnp.int32)[:, None]
    queries_t, grads_t = queries.T, grad_out.T

    near = reach // 2 + 1
    out, dq, far_grads, kept = first_call(
        starts, queries, queries_t, grad_out, grads_t, window, near, pack, head_count, score_scale
    )
    moved = ring_shift(far_grads, -(reach // 2))
    dq, near_grads = later_call(
        queries_t, grad_out, grads_t, out, kept, dq, window[1:near], 1, pack, head_count, 1.0, False
    )
    near_grads = (near_grads + moved.astype(jnp.float32)).astype(jnp.bfloat16)
    while near_grads.shape[0] > 2:
        half = near_grads.shape[0] // 2
        back = ring_shift(near_grads[half:], -half)
        near_grads = (near_grads[:half].astype(jnp.float32) + back.astype(jnp.float32)).astype(jnp.bfloat16)
    received = [ring_shift(near_grads[i], -1 - i) for i in range(near_grads.shape[0])]
    dq, own_grads = later_call(
        queries_t, grad_out, grads_t, out, kept, dq, window[:1], 0, pack, head_count, score_scale, True
    )
    total = own_grads[0]
    for part in received:
        total = total + part.astype(jnp.float32)
    grad_keys = (score_scale * total[:width]).astype(jnp.bfloat16).T
    grad_values = total[width:].astype(jnp.bfloat16).T
    return (out, dq, grad_keys, grad_values)


def solution(mesh):
    rows = P(("dp", "seq"), None)
    return jax.shard_map(
        shards,
        mesh=mesh,
        in_specs=(rows, rows, rows, P("dp"), rows),
        out_specs=(rows, rows, rows, rows),
        check_vma=False,
    )
```

time: 79.7 us -> 53.7 us (0.67)
  Pallas kernels: 35.2 us -> 22.9 us
  starting transfers between devices: 18.3 us -> 10.3 us
  waiting for transfers between devices: 16 us -> 8.97 us
  local copies, waits for them, and re-layouts: 6.18 us -> 9.44 us
  other arithmetic: 2.84 us -> 1.03 us
    pallas_call x1 -> x3, Pallas kernels: 35.2 us -> 22.9 us  [the longest x1 14.5 us: first_call(): pl.pallas_call(functools.partial(first_kernel, slot_count, near, pack, he...]
    ppermute x6 -> x7, starting transfers between devices: 18.3 us -> 10.3 us  [ring_shift(): lax.ppermute(value, 'seq', [(i, (i + steps) % count) for i in range(count)])]
    ppermute x6 -> x7, waiting for transfers between devices: 16 us -> 8.97 us  [ring_shift(): lax.ppermute(value, 'seq', [(i, (i + steps) % count) for i in range(count)])]
    unnamed x13, local copies, waits for them, and re-layouts: 5.13 us -> 7.76 us
    concatenate x1 -> x0, other arithmetic: 1.06 us -> none  [shards(): window = jnp.concatenate([own[None], window], axis=0)]
    another operation x3 -> x1, other arithmetic: 1.63 us -> 0.83 us
  transfers between devices with their start and end apart: 6 -> 7, of which waited for: 5 -> 5; matrix products, arithmetic and copies ran while one was open for 5% -> 7% of each run, Pallas kernels for 0% -> 16%
where the time goes in v1:
time: 53.7 us; the launch traced here: 53.4 us
  Pallas kernels  22.9 us (43%)
  starting transfers between devices  10.3 us (19%)
  local copies, waits for them, and re-layouts  9.44 us (18%)
  waiting for transfers between devices  8.97 us (17%)
  other arithmetic  1.03 us (2%)
  between operations  0.72 us (1%)
    pallas_call x1, Pallas kernels, first_call(): pl.pallas_call(functools.partial(first_kernel, slot_count, near, pack, he...  14.5 us
    ppermute x7, starting transfers between devices, ring_shift(): lax.ppermute(value, 'seq', [(i, (i + steps) % count) for i in range(count)])  10.3 us
    ppermute x7, waiting for transfers between devices, ring_shift(): lax.ppermute(value, 'seq', [(i, (i + steps) % count) for i in range(count)])  8.97 us
    pallas_call x2, Pallas kernels, later_call(): pl.pallas_call(functools.partial(later_kernel, first_slot, slots, pack, h...  8.44 us
    unnamed x13, local copies, waits for them, and re-layouts  7.76 us
  transfers between devices with their start and end apart: 7, of which 5 were waited for; matrix products, arithmetic and copies ran while one was open for 7% of the time, Pallas kernels for 16%

profile of v1, /device:TPU:0, one launch (start us, length us, event | category | flops | bytes accessed | tf_op | source)
XLA Modules:
  0.0 53.4 jit_solution(5004959061841973070)
XLA Ops:
  0.6 0.9 %constant_dynamic-update-slice_fusion.1 = bf16[512,128]{1,0:T(8,128)(2,1)S(1)} fusion(bf16[256,128]{1,0:T(8,128)(2,1)} %param.6), kind=kLoop, calls=%fused_computation.12 | loop fusion | bytes 131072
  1.6 0.9 %constant_dynamic-update-slice_fusion.refs_5_.refs_6_ = bf16[512,128]{1,0:T(8,128)(2,1)S(1)} fusion(bf16[512,128]{1,0:T(8,128)(2,1)S(1)} %constant_dynamic-update-slice_fusion.1, bf16[256,128]{1,0:T(8,128)(2,1)} %param.7), kind=kLoop, calls=%fused_computation.11 | loop fusion | bytes 131072 | tf_op jit(solution)/shard_map/concatenate | solution.py:207
  2.4 3.1 %collective-permute-start.1 = (bf16[512,128]{1,0:T(8,128)(2,1)S(1)}, bf16[512,128]{1,0:T(8,128)(2,1)S(1)}, u32[]{:S(2)}, u32[]{:S(2)}) collective-permute-start(bf16[512,128]{1,0:T(8,128)(2,1)S(1)} %constant_dynamic-update-slice_fusion.refs_5_.refs_6_), channel_id=1, source_target_pairs={{0,8},{4,12},{8,16},{12,20},{16,24},{20,28},{24,0},{28,4},{1,9},{5... | collective-permute-start | bytes 393224 | tf_op jit(solution)/shard_map/ppermute | solution.py:17
  5.5 1.5 %collective-permute-start = (bf16[512,128]{1,0:T(8,128)(2,1)S(1)}, bf16[512,128]{1,0:T(8,128)(2,1)S(1)}, u32[]{:S(2)}, u32[]{:S(2)}) collective-permute-start(bf16[512,128]{1,0:T(8,128)(2,1)S(1)} %constant_dynamic-update-slice_fusion.refs_5_.refs_6_), channel_id=1, source_target_pairs={{0,4},{4,8},{8,12},{12,16},{16,20},{20,24},{24,28},{28,0},{1,5},{5... | collective-permute-start | bytes 393224 | tf_op jit(solution)/shard_map/ppermute | solution.py:17
  7.1 0.8 %reduce-window.8 = s32[8,1]{0,1:T(1,128)S(1)} reduce-window(s32[8,1]{0,1:T(1,128)} %bitcast.25, s32[]{:T(128)} %constant.6.clone.1), window={size=8x1 pad=7_0x0_0}, to_apply=%region_0.0 | reduce-window | flops 56 | bytes 68 | tf_op jit(solution)/shard_map/reduce-window.3
  8.0 3.1 %collective-permute-done.1.refs_7_ = bf16[512,128]{1,0:T(8,128)(2,1)S(1)} collective-permute-done((bf16[512,128]{1,0:T(8,128)(2,1)S(1)}, bf16[512,128]{1,0:T(8,128)(2,1)S(1)}, u32[]{:S(2)}, u32[]{:S(2)}) %collective-permute-start.1) | collective-permute-done | bytes 131104 | tf_op jit(solution)/shard_map/ppermute | solution.py:17
  11.1 2.6 %collective-permute-start.2 = (bf16[512,128]{1,0:T(8,128)(2,1)S(1)}, bf16[512,128]{1,0:T(8,128)(2,1)}, u32[]{:S(2)}, u32[]{:S(2)}) collective-permute-start(bf16[512,128]{1,0:T(8,128)(2,1)S(1)} %collective-permute-done.1.refs_7_), channel_id=1, source_target_pairs={{0,4},{4,8},{8,12},{12,16},{16,20},{20,24},{24,28},{28,0},{1,5},{5... | collective-permute-start | bytes 393224 | tf_op jit(solution)/shard_map/ppermute | solution.py:17
  13.6 0.8 %copy.20.refs_0_ = s32[256,1]{1,0:T(8,128)} copy(s32[256,1]{0,1:T(1,128)S(1)} %bitcast.23) | data formatting | bytes 2048 | tf_op jit(solution)/shard_map/sub | solution.py:227
  14.5 1.5 %copy.18 = bf16[256,2048]{0,1:T(8,128)(2,1)S(1)} copy(bf16[256,2048]{1,0:T(8,128)(2,1)} %refs_1_.3) | data formatting | bytes 2097152 | tf_op args[0]
  15.9 0.5 copy.19
  16.5 1.4 %collective-permute-done.3.refs_9_ = bf16[512,128]{1,0:T(8,128)(2,1)} collective-permute-done((bf16[512,128]{1,0:T(8,128)(2,1)S(1)}, bf16[512,128]{1,0:T(8,128)(2,1)}, u32[]{:S(2)}, u32[]{:S(2)}) %collective-permute-start.3) | collective-permute-done | bytes 131104 | tf_op jit(solution)/shard_map/ppermute | solution.py:17
  17.9 3.4 %collective-permute-done.2.refs_8_ = bf16[512,128]{1,0:T(8,128)(2,1)} collective-permute-done((bf16[512,128]{1,0:T(8,128)(2,1)S(1)}, bf16[512,128]{1,0:T(8,128)(2,1)}, u32[]{:S(2)}, u32[]{:S(2)}) %collective-permute-start.2) | collective-permute-done | bytes 131104 | tf_op jit(solution)/shard_map/ppermute | solution.py:17
  21.4 1.2 %copy-done.2 = bf16[256,2048]{1,0:T(8,128)(2,1)S(1)} copy-done((bf16[256,2048]{1,0:T(8,128)(2,1)S(1)}, bf16[256,2048]{1,0:T(8,128)(2,1)}, u32[]{:S(2)}) %copy-start.2) | copy-done | bytes 1048600
  22.6 0.9 %copy-done.3 = s32[256,1]{1,0:T(8,128)S(1)} copy-done((s32[256,1]{1,0:T(8,128)S(1)}, s32[256,1]{1,0:T(8,128)}, u32[]{:S(2)}) %copy-start.3) | copy-done | bytes 1048
  23.5 14.5 %forward_far.1 = (bf16[256,2048]{1,0:T(8,128)(2,1)}, f32[256,2048]{1,0:T(8,128)S(1)}, bf16[2,256,256]{2,1,0:T(8,128)(2,1)S(1)}, bf16[3,4096,256]{2,1,0:T(8,128)(2,1)S(1)}) custom-call(s32[256,1]{1,0:T(8,128)S(1)} %copy-done.3, bf16[256,2048]{1,0:T(8,128)(2,1)S(1)} %copy-done.2, bf16[2048,256]{1,0:T(8,128)(2,1)S(1)} %bitcast.17, ...), custom_call_target="tpu_custom_call" | custom-call | tf_op jit(solution)/shard_map/forward_far/pallas_call | solution.py:161
  37.9 0.9 %collective-permute-start.4 = (bf16[2,256,256]{2,1,0:T(8,128)(2,1)S(1)}, bf16[2,256,256]{2,1,0:T(8,128)(2,1)S(1)}, u32[]{:S(2)}, u32[]{:S(2)}) collective-permute-start(bf16[2,256,256]{2,1,0:T(8,128)(2,1)S(1)} %get-tuple-element.19), channel_id=1, source_target_pairs={{0,24},{4,28},{8,0},{12,4},{16,8},{20,12},{24,16},{28,20},{1,25},{... | collective-permute-start | bytes 786440 | tf_op jit(solution)/shard_map/ppermute | solution.py:17
  38.9 1.2 %copy-done.1 = bf16[256,2048]{1,0:T(8,128)(2,1)S(1)} copy-done((bf16[256,2048]{1,0:T(8,128)(2,1)S(1)}, bf16[256,2048]{1,0:T(8,128)(2,1)}, u32[]{:S(2)}) %copy-start.1) | copy-done | bytes 1048600
  40.1 4.6 %backward_near.2 = (f32[256,2048]{1,0:T(8,128)S(1)}, f32[2,256,256]{2,1,0:T(8,128)S(1)}) custom-call(bf16[2048,256]{1,0:T(8,128)(2,1)S(1)} %bitcast.18, bf16[256,2048]{1,0:T(8,128)(2,1)S(1)} %copy-done, bf16[2048,256]{1,0:T(8,128)(2,1)S(1)} %bitcast.21, bf16[256,2048]{1,0:T(8,128)(2,1)S(1)} %copy-done.1, ...), custom_call_target="tpu_custom_call" | custom-call | tf_op jit(solution)/shard_map/backward_near/pallas_call | solution.py:185
  45.1 1.8 %collective-permute-start.5 = (bf16[256,256]{1,0:T(8,128)(2,1)S(1)}, bf16[256,256]{1,0:T(8,128)(2,1)S(1)}, u32[]{:S(2)}, u32[]{:S(2)}) collective-permute-start(bf16[256,256]{1,0:T(8,128)(2,1)S(1)} %get-tuple-element.32), channel_id=1, source_target_pairs={{0,28},{4,0},{8,4},{12,8},{16,12},{20,16},{24,20},{28,24},{1,29},{... | collective-permute-start | bytes 393224 | tf_op jit(solution)/shard_map/ppermute | solution.py:17
  46.9 0.4 collective-permute-start.6
  47.2 3.9 %backward_near.3 = (bf16[256,2048]{1,0:T(8,128)(2,1)}, f32[1,256,256]{2,1,0:T(8,128)S(1)}) custom-call(bf16[2048,256]{1,0:T(8,128)(2,1)S(1)} %bitcast.19, bf16[256,2048]{1,0:T(8,128)(2,1)S(1)} %copy-done, bf16[2048,256]{1,0:T(8,128)(2,1)S(1)} %bitcast.22, bf16[256,2048]{1,0:T(8,128)(2,1)S(1)} %copy-done.1, ...), custom_call_target="tpu_custom_call" | custom-call | tf_op jit(solution)/shard_map/backward_near/pallas_call | solution.py:185
  51.1 0.7 %collective-permute-done.6 = bf16[256,256]{1,0:T(8,128)(2,1)S(1)} collective-permute-done((bf16[256,256]{1,0:T(8,128)(2,1)S(1)}, bf16[256,256]{1,0:T(8,128)(2,1)S(1)}, u32[]{:S(2)}, u32[]{:S(2)}) %collective-permute-start.6) | collective-permute-done | bytes 131104 | tf_op jit(solution)/shard_map/ppermute | solution.py:17
  51.9 0.7 %copy.21 = bf16[256,128]{1,0:T(8,128)(2,1)} copy(bf16[256,128]{0,1:T(8,128)(2,1)S(1)} %fusion.2) | data formatting | bytes 131072
  52.6 0.7 %copy.22 = bf16[256,128]{1,0:T(8,128)(2,1)} copy(bf16[256,128]{0,1:T(8,128)(2,1)S(1)} %fusion.3) | data formatting | bytes 131072
  (17 shorter events, 0.6 us)
Async XLA Ops:
  0.6 15.3 %copy-start = (bf16[256,2048]{1,0:T(8,128)(2,1)S(1)}, bf16[256,2048]{1,0:T(8,128)(2,1)}, u32[]{:S(2)}) copy-start(bf16[256,2048]{1,0:T(8,128)(2,1)} %refs_1_.5) | copy-start | bytes 3145732
  2.4 8.6 %collective-permute-start.1 = (bf16[512,128]{1,0:T(8,128)(2,1)S(1)}, bf16[512,128]{1,0:T(8,128)(2,1)S(1)}, u32[]{:S(2)}, u32[]{:S(2)}) collective-permute-start(bf16[512,128]{1,0:T(8,128)(2,1)S(1)} %constant_dynamic-update-slice_fusion.refs_5_.refs_6_), channel_id=1, source_target_pairs={{0,8},{4,12},{8,16},{12,20},{16,24},{20,28},{24,0},{28,4},{1,9},{5... | collective-permute-start | bytes 393224 | tf_op jit(solution)/shard_map/ppermute | solution.py:17
  5.5 10.9 %collective-permute-start = (bf16[512,128]{1,0:T(8,128)(2,1)S(1)}, bf16[512,128]{1,0:T(8,128)(2,1)S(1)}, u32[]{:S(2)}, u32[]{:S(2)}) collective-permute-start(bf16[512,128]{1,0:T(8,128)(2,1)S(1)} %constant_dynamic-update-slice_fusion.refs_5_.refs_6_), channel_id=1, source_target_pairs={{0,4},{4,8},{8,12},{12,16},{16,20},{20,24},{24,28},{28,0},{1,5},{5... | collective-permute-start | bytes 393224 | tf_op jit(solution)/shard_map/ppermute | solution.py:17
  11.1 6.9 %collective-permute-start.3 = (bf16[512,128]{1,0:T(8,128)(2,1)S(1)}, bf16[512,128]{1,0:T(8,128)(2,1)}, u32[]{:S(2)}, u32[]{:S(2)}) collective-permute-start(bf16[512,128]{1,0:T(8,128)(2,1)S(1)} %collective-permute-done.1.refs_7_), channel_id=1, source_target_pairs={{0,8},{4,12},{8,16},{12,20},{16,24},{20,28},{24,0},{28,4},{1,9},{5... | collective-permute-start | bytes 393224 | tf_op jit(solution)/shard_map/ppermute | solution.py:17
  11.1 10.3 %collective-permute-start.2 = (bf16[512,128]{1,0:T(8,128)(2,1)S(1)}, bf16[512,128]{1,0:T(8,128)(2,1)}, u32[]{:S(2)}, u32[]{:S(2)}) collective-permute-start(bf16[512,128]{1,0:T(8,128)(2,1)S(1)} %collective-permute-done.1.refs_7_), channel_id=1, source_target_pairs={{0,4},{4,8},{8,12},{12,16},{16,20},{20,24},{24,28},{28,0},{1,5},{5... | collective-permute-start | bytes 393224 | tf_op jit(solution)/shard_map/ppermute | solution.py:17
  21.4 1.2 %copy-start.2 = (bf16[256,2048]{1,0:T(8,128)(2,1)S(1)}, bf16[256,2048]{1,0:T(8,128)(2,1)}, u32[]{:S(2)}) copy-start(bf16[256,2048]{1,0:T(8,128)(2,1)} %refs_1_.3) | copy-start | bytes 3145732
  22.6 0.9 %copy-start.3 = (s32[256,1]{1,0:T(8,128)S(1)}, s32[256,1]{1,0:T(8,128)}, u32[]{:S(2)}) copy-start(s32[256,1]{1,0:T(8,128)} %copy.20.refs_0_) | copy-start | bytes 3076
  37.9 7.0 %collective-permute-start.4 = (bf16[2,256,256]{2,1,0:T(8,128)(2,1)S(1)}, bf16[2,256,256]{2,1,0:T(8,128)(2,1)S(1)}, u32[]{:S(2)}, u32[]{:S(2)}) collective-permute-start(bf16[2,256,256]{2,1,0:T(8,128)(2,1)S(1)} %get-tuple-element.19), channel_id=1, source_target_pairs={{0,24},{4,28},{8,0},{12,4},{16,8},{20,12},{24,16},{28,20},{1,25},{... | collective-permute-start | bytes 786440 | tf_op jit(solution)/shard_map/ppermute | solution.py:17
  38.9 1.2 %copy-start.1 = (bf16[256,2048]{1,0:T(8,128)(2,1)S(1)}, bf16[256,2048]{1,0:T(8,128)(2,1)}, u32[]{:S(2)}) copy-start(bf16[256,2048]{1,0:T(8,128)(2,1)} %get-tuple-element.28.refs_3_) | copy-start | bytes 3145732
  45.1 6.1 %collective-permute-start.5 = (bf16[256,256]{1,0:T(8,128)(2,1)S(1)}, bf16[256,256]{1,0:T(8,128)(2,1)S(1)}, u32[]{:S(2)}, u32[]{:S(2)}) collective-permute-start(bf16[256,256]{1,0:T(8,128)(2,1)S(1)} %get-tuple-element.32), channel_id=1, source_target_pairs={{0,28},{4,0},{8,4},{12,8},{16,12},{20,16},{24,20},{28,24},{1,29},{... | collective-permute-start | bytes 393224 | tf_op jit(solution)/shard_map/ppermute | solution.py:17
  46.9 5.0 %collective-permute-start.6 = (bf16[256,256]{1,0:T(8,128)(2,1)S(1)}, bf16[256,256]{1,0:T(8,128)(2,1)S(1)}, u32[]{:S(2)}, u32[]{:S(2)}) collective-permute-start(bf16[256,256]{1,0:T(8,128)(2,1)S(1)} %get-tuple-element.33), channel_id=1, source_target_pairs={{0,24},{4,28},{8,0},{12,4},{16,8},{20,12},{24,16},{28,20},{1,25},{... | collective-permute-start | bytes 393224 | tf_op jit(solution)/shard_map/ppermute | solution.py:17

commit v2 on v1

--- a/solution.py
+++ b/solution.py
@@ -71,21 +71,66 @@
     return split_chain(steps, [kv_ref[:tokens] for kv_ref in kv_refs], 2)
 
 
+def join_kernel(keys_ref, values_ref, own_ref, sems):
+    tokens = keys_ref.shape[0]
+    copies = [
+        pltpu.make_async_copy(keys_ref, own_ref.at[pl.ds(0, tokens)], sems.at[0]),
+        pltpu.make_async_copy(values_ref, own_ref.at[pl.ds(tokens, tokens)], sems.at[1]),
+    ]
+    for copy in copies:
+        copy.start()
+    for copy in copies:
+        copy.wait()
+
+
+def prepare_kernel(
+    slot_count, lengths_ref, q_in, g_in, q_ref, g_ref, qt_ref, gt_ref, bias_ref, sems
+):
+    tokens = q_ref.shape[0]
+    copies = [
+        pltpu.make_async_copy(q_in, q_ref, sems.at[0]),
+        pltpu.make_async_copy(g_in, g_ref, sems.at[1]),
+    ]
+    for copy in copies:
+        copy.start()
+    first = lax.axis_index("seq") * tokens
+    row = lax.broadcasted_iota(jnp.int32, (tokens, tokens), 0)
+    lane = lax.broadcasted_iota(jnp.int32, (tokens, tokens), 1)
+    row_start = jnp.full((tokens, tokens), -first, jnp.int32)
+    end = -first
+    for document in range(lengths_ref.shape[0]):
+        end = end + lengths_ref[document]
+        row_start = jnp.where(row >= end, end, row_start)
+    for slot in range(slot_count):
+        visible = lane - slot * tokens >= row_start
+        if slot == 0:
+            visible = visible & (lane <= row)
+        bias_ref[slot] = jnp.where(visible, 0.0, NEG_FILL)
+    copies[0].wait()
+    qt_ref[...] = q_ref[...].T
+    copies[1].wait()
+    gt_ref[...] = g_ref[...].T
+
+
+def finish_kernel(score_scale, own_ref, *refs):
+    part_refs, (keys_ref, values_ref) = refs[:-2], refs[-2:]
+    width = keys_ref.shape[1]
+    total = own_ref[0]
+    for part_ref in part_refs:
+        total = total + part_ref[...].astype(jnp.float32)
+    keys_ref[...] = (score_scale * total[:width]).T.astype(jnp.bfloat16)
+    values_ref[...] = total[width:].T.astype(jnp.bfloat16)
+
+
 def first_kernel(slot_count, near, pack, head_count, score_scale, *refs):
-    start_ref, q_ref, qt_ref, g_ref, gt_ref = refs[:5]
+    bias_ref, q_ref, qt_ref, g_ref, gt_ref = refs[:5]
     kv_refs = refs[5 : 5 + slot_count]
-    out_ref, dq_ref, grad_out_ref, kept_ref, bias_ref, vext_ref, grad_ref = refs[5 + slot_count :]
+    out_ref, dq_ref, grad_out_ref, kept_ref, delta_ref, vext_ref, grad_ref = refs[5 + slot_count :]
     tokens = q_ref.shape[0]
     width = q_ref.shape[1] // head_count
     rows = pack * tokens
     factor = score_scale * LOG2_E
-    row_start = start_ref[...]
     for slot in range(slot_count):
-        key_pos = lax.broadcasted_iota(jnp.int32, (tokens, tokens), 1) - slot * tokens
-        visible = key_pos >= row_start
-        if slot == 0:
-            visible = visible & (key_pos <= lax.broadcasted_iota(jnp.int32, (tokens, tokens), 0))
-        bias_ref[slot] = jnp.where(visible, 0.0, NEG_FILL)
         vext_ref[slot, :, :width] = kv_refs[slot][tokens:]
         vext_ref[slot, :, width:] = jnp.ones((tokens, width), jnp.bfloat16)
     grad_ref[...] = jnp.zeros(grad_ref.shape, jnp.float32)
@@ -110,6 +155,7 @@
         inverse = jnp.concatenate([inverse] * (tokens // width), axis=1)
         weights = [(w.astype(jnp.float32) * inverse).astype(jnp.bfloat16) for w in weights]
         group_rows = pl.ds(pl.multiple_of(group * rows, rows), rows)
+        delta_ref[group_rows] = jnp.broadcast_to(delta, (rows, width))
         for slot in range(near):
             kept_ref[slot, group_rows] = weights[slot]
         q_t = take_columns(qt_ref, group, pack, width)
@@ -125,7 +171,7 @@
 
 
 def later_kernel(first_slot, slots, pack, head_count, dq_scale, *refs):
-    qt_ref, g_ref, gt_ref, out_ref, kept_ref, dq_in_ref = refs[:6]
+    qt_ref, g_ref, gt_ref, delta_ref, kept_ref, dq_in_ref = refs[:6]
     kv_refs = refs[6 : 6 + slots]
     dq_ref, grad_ref = refs[6 + slots :]
     tokens = g_ref.shape[0]
@@ -135,8 +181,8 @@
 
     def one_group(group, carry):
         g = take_rows(g_ref, group, pack, width)
-        delta = row_dots(g, take_rows(out_ref, group, pack, width))
         group_rows = pl.ds(pl.multiple_of(group * rows, rows), rows)
+        delta = jnp.concatenate([delta_ref[group_rows]] * (tokens // width), axis=1)
         weights = [kept_ref[first_slot + index, group_rows] for index in range(slots)]
         q_t = take_columns(qt_ref, group, pack, width)
         g_t = take_columns(gt_ref, group, pack, width)
@@ -151,9 +197,58 @@
 
 
 VMEM = pl.BlockSpec(memory_space=pltpu.VMEM)
-
-
-def first_call(start, q, qt, g, gt, kvs, near, pack, head_count, score_scale):
+HBM = pl.BlockSpec(memory_space=pltpu.HBM)
+
+
+def in_hbm(value):
+    return pltpu.with_memory_space_constraint(value, pltpu.HBM)
+
+
+def join_call(keys, values):
+    return pl.pallas_call(
+        join_kernel,
+        out_shape=jax.ShapeDtypeStruct((2 * keys.shape[0], keys.shape[1]), keys.dtype),
+        in_specs=[HBM] * 2,
+        out_specs=VMEM,
+        scratch_shapes=[pltpu.SemaphoreType.DMA((2,))],
+        compiler_params=pltpu.CompilerParams(vmem_limit_bytes=1 << 20),
+        name="join",
+    )(in_hbm(keys), in_hbm(values))
+
+
+def prepare_call(lengths, q, g, slot_count):
+    tokens, lanes = q.shape
+    return pl.pallas_call(
+        functools.partial(prepare_kernel, slot_count),
+        out_shape=(
+            jax.ShapeDtypeStruct(q.shape, q.dtype),
+            jax.ShapeDtypeStruct(g.shape, g.dtype),
+            jax.ShapeDtypeStruct((lanes, tokens), q.dtype),
+            jax.ShapeDtypeStruct((lanes, tokens), g.dtype),
+            jax.ShapeDtypeStruct((slot_count, tokens, tokens), jnp.float32),
+        ),
+        in_specs=[pl.BlockSpec(memory_space=pltpu.SMEM), HBM, HBM],
+        out_specs=(VMEM,) * 5,
+        scratch_shapes=[pltpu.SemaphoreType.DMA((2,))],
+        compiler_params=pltpu.CompilerParams(vmem_limit_bytes=2 << 20),
+        name="prepare",
+    )(in_hbm(lengths), in_hbm(q), in_hbm(g))
+
+
+def finish_call(own, parts, score_scale, width):
+    tokens = own.shape[2]
+    shape = jax.ShapeDtypeStruct((tokens, width), jnp.bfloat16)
+    return pl.pallas_call(
+        functools.partial(finish_kernel, score_scale),
+        out_shape=(shape, shape),
+        in_specs=[VMEM] * (1 + len(parts)),
+        out_specs=(VMEM,) * 2,
+        compiler_params=pltpu.CompilerParams(vmem_limit_bytes=1 << 20),
+        name="finish",
+    )(own, *parts)
+
+
+def first_call(bias, q, qt, g, gt, kvs, near, pack, head_count, score_scale):
     slot_count = len(kvs)
     tokens = q.shape[0]
     width = q.shape[1] // head_count
@@ -165,20 +260,20 @@
             jax.ShapeDtypeStruct(q.shape, jnp.float32),
             jax.ShapeDtypeStruct((far, 2 * width, tokens), jnp.bfloat16),
             jax.ShapeDtypeStruct((near, head_count * tokens, tokens), jnp.bfloat16),
+            jax.ShapeDtypeStruct((head_count * tokens, width), jnp.float32),
         ),
         in_specs=[VMEM] * (5 + slot_count),
-        out_specs=(VMEM,) * 4,
+        out_specs=(VMEM,) * 5,
         scratch_shapes=[
-            pltpu.VMEM((slot_count, tokens, tokens), jnp.float32),
             pltpu.VMEM((slot_count, tokens, 2 * width), jnp.bfloat16),
             pltpu.VMEM((far, 2 * width, tokens), jnp.float32),
         ],
-        compiler_params=pltpu.CompilerParams(vmem_limit_bytes=40 << 20),
+        compiler_params=pltpu.CompilerParams(vmem_limit_bytes=slot_count * (5 << 20)),
         name="forward_far",
-    )(start, q, qt, g, gt, *kvs)
-
-
-def later_call(qt, g, gt, out, kept, dq, kvs, first_slot, pack, head_count, dq_scale, last):
+    )(bias, q, qt, g, gt, *kvs)
+
+
+def later_call(qt, g, gt, delta, kept, dq, kvs, first_slot, pack, head_count, dq_scale, last):
     slots = len(kvs)
     tokens = g.shape[0]
     width = g.shape[1] // head_count
@@ -190,21 +285,19 @@
         ),
         in_specs=[VMEM] * (6 + slots),
         out_specs=(VMEM,) * 2,
-        compiler_params=pltpu.CompilerParams(vmem_limit_bytes=24 << 20),
+        compiler_params=pltpu.CompilerParams(vmem_limit_bytes=slots * (3 << 20)),
         name="backward_near",
-    )(qt, g, gt, out, kept, dq, *kvs)
+    )(qt, g, gt, delta, kept, dq, *kvs)
 
 
 def shards(queries, keys, values, lengths, grad_out):
-    tokens = queries.shape[0]
     width = keys.shape[1]
     head_count = queries.shape[1] // width
     reach = min(8, lax.axis_size("seq") // 2)
-    rank = lax.axis_index("seq")
     score_scale = 1.0 / math.sqrt(width)
     pack = math.gcd(8, head_count)
 
-    own = jnp.concatenate([keys, values], axis=0)
+    own = join_call(keys, values)
     window = [own]
     if reach > 1:
         two = ring_shift(own, 2)
@@ -220,20 +313,17 @@
         shift = len(window) - 1
         window += [ring_shift(part, shift) for part in window[1:]]
 
-    first = rank * tokens
-    positions = first + jnp.arange(tokens, dtype=jnp.int32)
-    doc_ends = jnp.cumsum(lengths)
-    starts = jnp.max(jnp.where(doc_ends[None, :] <= positions[:, None], doc_ends[None, :], 0), axis=1)
-    starts = (starts - first).astype(jnp.int32)[:, None]
-    queries_t, grads_t = queries.T, grad_out.T
+    queries, grad_out, queries_t, grads_t, bias = prepare_call(
+        lengths, queries, grad_out, reach + 1
+    )
 
     near = reach // 2 + 1
-    out, dq, far_grads, kept = first_call(
-        starts, queries, queries_t, grad_out, grads_t, window, near, pack, head_count, score_scale
+    out, dq, far_grads, kept, delta = first_call(
+        bias, queries, queries_t, grad_out, grads_t, window, near, pack, head_count, score_scale
     )
     moved = ring_shift(far_grads, -(reach // 2))
     dq, near_grads = later_call(
-        queries_t, grad_out, grads_t, out, kept, dq, window[1:near], 1, pack, head_count, 1.0, False
+        queries_t, grad_out, grads_t, delta, kept, dq, window[1:near], 1, pack, head_count, 1.0, False
     )
     near_grads = (near_grads + moved.astype(jnp.float32)).astype(jnp.bfloat16)
     while near_grads.shape[0] > 2:
@@ -242,13 +332,9 @@
         near_grads = (near_grads[:half].astype(jnp.float32) + back.astype(jnp.float32)).astype(jnp.bfloat16)
     received = [ring_shift(near_grads[i], -1 - i) for i in range(near_grads.shape[0])]
     dq, own_grads = later_call(
-        queries_t, grad_out, grads_t, out, kept, dq, window[:1], 0, pack, head_count, score_scale, True
-    )
-    total = own_grads[0]
-    for part in received:
-        total = total + part.astype(jnp.float32)
-    grad_keys = (score_scale * total[:width]).astype(jnp.bfloat16).T
-    grad_values = total[width:].astype(jnp.bfloat16).T
+        queries_t, grad_out, grads_t, delta, kept, dq, window[:1], 0, pack, head_count, score_scale, True
+    )
+    grad_keys, grad_values = finish_call(own_grads, received, score_scale, width)
     return (out, dq, grad_keys, grad_values)
 
 

time: 53.7 us -> 49.3 us (0.918)
  local copies, waits for them, and re-layouts: 9.44 us -> 0.02 us
  Pallas kernels: 22.9 us -> 26.3 us
  waiting for transfers between devices: 8.97 us -> 11.5 us
  other arithmetic: 1.03 us -> 0.06 us
    unnamed x13 -> x0, local copies, waits for them, and re-layouts: 7.76 us -> none
    pallas_call x0 -> x3, Pallas kernels: none -> 4.21 us  [the longest x1 2.56 us: prepare_call(): pl.pallas_call(functools.partial(prepare_kernel, slot_count), out_shape=(...]
    ppermute x7, waiting for transfers between devices: 8.97 us -> 11.5 us  [ring_shift(): lax.ppermute(value, 'seq', [(i, (i + steps) % count) for i in range(count)])]
    concatenate x1 -> x0, local copies, waits for them, and re-layouts: 0.85 us -> none  [shards(): own = jnp.concatenate([keys, values], axis=0)]
    another operation x1 -> x0, other arithmetic: 0.83 us -> none
    sub x1 -> x0, local copies, waits for them, and re-layouts: 0.8 us -> none  [shards(): starts = (starts - first).astype(jnp.int32)[:, None]]
    pallas_call x1, Pallas kernels: 14.5 us -> 13.7 us  [first_call(): pl.pallas_call(functools.partial(first_kernel, slot_count, near, pack, he...]
  transfers between devices with their start and end apart: 7 -> 7, of which waited for: 5 -> 5; matrix products, arithmetic and copies ran while one was open for 7% -> 0% of each run, Pallas kernels for 16% -> 22%
where the time goes in v2:
time: 49.3 us; the launch traced here: 49.1 us
  Pallas kernels  26.3 us (53%)
  waiting for transfers between devices  11.5 us (23%)
  starting transfers between devices  10.4 us (21%)
  between operations  0.68 us (1%)
    pallas_call x1, Pallas kernels, first_call(): pl.pallas_call(functools.partial(first_kernel, slot_count, near, pack, he...  13.7 us
    ppermute x7, waiting for transfers between devices, ring_shift(): lax.ppermute(value, 'seq', [(i, (i + steps) % count) for i in range(count)])  11.5 us
    ppermute x7, starting transfers between devices, ring_shift(): lax.ppermute(value, 'seq', [(i, (i + steps) % count) for i in range(count)])  10.4 us
    pallas_call x2, Pallas kernels, later_call(): pl.pallas_call(functools.partial(later_kernel, first_slot, slots, pack, h...  8.41 us
    pallas_call x1, Pallas kernels, prepare_call(): pl.pallas_call(functools.partial(prepare_kernel, slot_count), out_shape=(...  2.56 us
  transfers between devices with their start and end apart: 7, of which 5 were waited for; matrix products, arithmetic and copies ran while one was open for 0% of the time, Pallas kernels for 22%

profile of v2, /device:TPU:0, one launch (start us, length us, event | category | flops | bytes accessed | tf_op | source)
XLA Modules:
  0.0 49.1 jit_solution(11533942867615362714)
XLA Ops:
  0.6 0.9 %join.1.refs_5_.refs_6_ = bf16[512,128]{1,0:T(8,128)(2,1)S(1)} custom-call(bf16[256,128]{1,0:T(8,128)(2,1)} %keys_ref.1, bf16[256,128]{1,0:T(8,128)(2,1)} %values_ref.1), custom_call_target="tpu_custom_call" | custom-call | tf_op jit(solution)/shard_map/join/pallas_call | solution.py:208
  1.5 3.1 %collective-permute-start.1 = (bf16[512,128]{1,0:T(8,128)(2,1)S(1)}, bf16[512,128]{1,0:T(8,128)(2,1)S(1)}, u32[]{:S(2)}, u32[]{:S(2)}) collective-permute-start(bf16[512,128]{1,0:T(8,128)(2,1)S(1)} %join.1.refs_5_.refs_6_), channel_id=1, source_target_pairs={{0,8},{4,12},{8,16},{12,20},{16,24},{20,28},{24,0},{28,4},{1,9},{5... | collective-permute-start | bytes 393224 | tf_op jit(solution)/shard_map/ppermute | solution.py:17
  4.6 1.5 %collective-permute-start = (bf16[512,128]{1,0:T(8,128)(2,1)S(1)}, bf16[512,128]{1,0:T(8,128)(2,1)S(1)}, u32[]{:S(2)}, u32[]{:S(2)}) collective-permute-start(bf16[512,128]{1,0:T(8,128)(2,1)S(1)} %join.1.refs_5_.refs_6_), channel_id=1, source_target_pairs={{0,4},{4,8},{8,12},{12,16},{16,20},{20,24},{24,28},{28,0},{1,5},{5... | collective-permute-start | bytes 393224 | tf_op jit(solution)/shard_map/ppermute | solution.py:17
  6.2 4.0 %collective-permute-done.1.refs_7_ = bf16[512,128]{1,0:T(8,128)(2,1)S(1)} collective-permute-done((bf16[512,128]{1,0:T(8,128)(2,1)S(1)}, bf16[512,128]{1,0:T(8,128)(2,1)S(1)}, u32[]{:S(2)}, u32[]{:S(2)}) %collective-permute-start.1) | collective-permute-done | bytes 131104 | tf_op jit(solution)/shard_map/ppermute | solution.py:17
  10.2 0.0 collective-permute-start.3
  10.2 2.6 %collective-permute-start.2 = (bf16[512,128]{1,0:T(8,128)(2,1)S(1)}, bf16[512,128]{1,0:T(8,128)(2,1)S(1)}, u32[]{:S(2)}, u32[]{:S(2)}) collective-permute-start(bf16[512,128]{1,0:T(8,128)(2,1)S(1)} %collective-permute-done.1.refs_7_), channel_id=1, source_target_pairs={{0,4},{4,8},{8,12},{12,16},{16,20},{20,24},{24,28},{28,0},{1,5},{5... | collective-permute-start | bytes 393224 | tf_op jit(solution)/shard_map/ppermute | solution.py:17
  12.7 2.6 %prepare.1 = (bf16[256,2048]{1,0:T(8,128)(2,1)S(1)}, bf16[256,2048]{1,0:T(8,128)(2,1)S(1)}, bf16[2048,256]{1,0:T(8,128)(2,1)S(1)}, bf16[2048,256]{1,0:T(8,128)(2,1)S(1)}, f32[5,256,256]{2,1,0:T(8,128)S(1)}) custom-call(s32[8]{0:T(128)} %lengths_ref.1, bf16[256,2048]{1,0:T(8,128)(2,1)} %q_in.1, bf16[256,2048]{1,0:T(8,128)(2,1)} %g_in.1), custom_call_target="tpu_custom_call" | custom-call | tf_op jit(solution)/shard_map/prepare/pallas_call | solution.py:221
  15.3 0.0 collective-permute-done.refs_6_
  15.3 1.6 %collective-permute-done.3.refs_9_ = bf16[512,128]{1,0:T(8,128)(2,1)S(1)} collective-permute-done((bf16[512,128]{1,0:T(8,128)(2,1)S(1)}, bf16[512,128]{1,0:T(8,128)(2,1)S(1)}, u32[]{:S(2)}, u32[]{:S(2)}) %collective-permute-start.3) | collective-permute-done | bytes 131104 | tf_op jit(solution)/shard_map/ppermute | solution.py:17
  16.9 3.4 %collective-permute-done.2.refs_8_ = bf16[512,128]{1,0:T(8,128)(2,1)S(1)} collective-permute-done((bf16[512,128]{1,0:T(8,128)(2,1)S(1)}, bf16[512,128]{1,0:T(8,128)(2,1)S(1)}, u32[]{:S(2)}, u32[]{:S(2)}) %collective-permute-start.2) | collective-permute-done | bytes 131104 | tf_op jit(solution)/shard_map/ppermute | solution.py:17
  20.4 13.7 %forward_far.1 = (bf16[256,2048]{1,0:T(8,128)(2,1)}, f32[256,2048]{1,0:T(8,128)S(1)}, bf16[2,256,256]{2,1,0:T(8,128)(2,1)S(1)}, bf16[3,4096,256]{2,1,0:T(8,128)(2,1)S(1)}, f32[4096,128]{1,0:T(8,128)S(1)}) custom-call(f32[5,256,256]{2,1,0:T(8,128)S(1)} %get-tuple-element.20.refs_0_, bf16[256,2048]{1,0:T(8,128)(2,1)S(1)} %get-tuple-element.21.refs_1_, ...), custom_call_target="tpu_custom_call" | custom-call | tf_op jit(solution)/shard_map/forward_far/pallas_call | solution.py:256
  34.1 0.9 %collective-permute-start.4 = (bf16[2,256,256]{2,1,0:T(8,128)(2,1)S(1)}, bf16[2,256,256]{2,1,0:T(8,128)(2,1)S(1)}, u32[]{:S(2)}, u32[]{:S(2)}) collective-permute-start(bf16[2,256,256]{2,1,0:T(8,128)(2,1)S(1)} %get-tuple-element.33), channel_id=1, source_target_pairs={{0,24},{4,28},{8,0},{12,4},{16,8},{20,12},{24,16},{28,20},{1,25},{... | collective-permute-start | bytes 786440 | tf_op jit(solution)/shard_map/ppermute | solution.py:17
  35.0 4.5 %backward_near.2 = (f32[256,2048]{1,0:T(8,128)S(1)}, f32[2,256,256]{2,1,0:T(8,128)S(1)}) custom-call(bf16[2048,256]{1,0:T(8,128)(2,1)S(1)} %get-tuple-element.22.refs_2_.refs_0_, bf16[256,2048]{1,0:T(8,128)(2,1)S(1)} %get-tuple-element.23.refs_3_.refs_1_, bf16[2048,256]{1,0:T(8,128)(2,1)S(1)} %get-tuple-element.24.refs_4_.refs_2_, ...), custom_call_target="tpu_custom_call" | custom-call | tf_op jit(solution)/shard_map/backward_near/pallas_call | solution.py:280
  39.5 1.4 %collective-permute-done.4 = bf16[2,256,256]{2,1,0:T(8,128)(2,1)S(1)} collective-permute-done((bf16[2,256,256]{2,1,0:T(8,128)(2,1)S(1)}, bf16[2,256,256]{2,1,0:T(8,128)(2,1)S(1)}, u32[]{:S(2)}, u32[]{:S(2)}) %collective-permute-start.4) | collective-permute-done | bytes 262176 | tf_op jit(solution)/shard_map/ppermute | solution.py:17
  40.9 0.1 add_convert_fusion
  41.0 2.3 %collective-permute-start.6 = (bf16[256,256]{1,0:T(8,128)(2,1)S(1)}, bf16[256,256]{1,0:T(8,128)(2,1)S(1)}, u32[]{:S(2)}, u32[]{:S(2)}) collective-permute-start(bf16[256,256]{1,0:T(8,128)(2,1)S(1)} %get-tuple-element.36), channel_id=1, source_target_pairs={{0,24},{4,28},{8,0},{12,4},{16,8},{20,12},{24,16},{28,20},{1,25},{... | collective-permute-start | bytes 393224 | tf_op jit(solution)/shard_map/ppermute | solution.py:17
  43.3 0.0 collective-permute-start.5
  43.3 3.9 %backward_near.3 = (bf16[256,2048]{1,0:T(8,128)(2,1)}, f32[1,256,256]{2,1,0:T(8,128)S(1)}) custom-call(bf16[2048,256]{1,0:T(8,128)(2,1)S(1)} %get-tuple-element.22.refs_2_.refs_0_, bf16[256,2048]{1,0:T(8,128)(2,1)S(1)} %get-tuple-element.23.refs_3_.refs_1_, bf16[2048,256]{1,0:T(8,128)(2,1)S(1)} %get-tuple-element.24.refs_4_.refs_2_, ...), custom_call_target="tpu_custom_call" | custom-call | tf_op jit(solution)/shard_map/backward_near/pallas_call | solution.py:280
  47.2 0.0 collective-permute-done.6.refs_1_
  47.2 1.1 %collective-permute-done.5.refs_0_ = bf16[256,256]{1,0:T(8,128)(2,1)S(1)} collective-permute-done((bf16[256,256]{1,0:T(8,128)(2,1)S(1)}, bf16[256,256]{1,0:T(8,128)(2,1)S(1)}, u32[]{:S(2)}, u32[]{:S(2)}) %collective-permute-start.5) | collective-permute-done | bytes 131104 | tf_op jit(solution)/shard_map/ppermute | solution.py:17
  48.3 0.8 %finish.1 = (bf16[256,128]{1,0:T(8,128)(2,1)}, bf16[256,128]{1,0:T(8,128)(2,1)}) custom-call(f32[1,256,256]{2,1,0:T(8,128)S(1)} %get-tuple-element.31.own_ref, bf16[256,256]{1,0:T(8,128)(2,1)S(1)} %collective-permute-done.5.refs_0_, bf16[256,256]{1,0:T(8,128)(2,1)S(1)} %collective-permute-done.6.refs_1_), custom_call_target="tpu_custom_call" | custom-call | tf_op jit(solution)/shard_map/finish/pallas_call | solution.py:241
  (1 shorter events, 0.0 us)
Async XLA Ops:
  1.5 8.6 %collective-permute-start.1 = (bf16[512,128]{1,0:T(8,128)(2,1)S(1)}, bf16[512,128]{1,0:T(8,128)(2,1)S(1)}, u32[]{:S(2)}, u32[]{:S(2)}) collective-permute-start(bf16[512,128]{1,0:T(8,128)(2,1)S(1)} %join.1.refs_5_.refs_6_), channel_id=1, source_target_pairs={{0,8},{4,12},{8,16},{12,20},{16,24},{20,28},{24,0},{28,4},{1,9},{5... | collective-permute-start | bytes 393224 | tf_op jit(solution)/shard_map/ppermute | solution.py:17
  4.6 10.7 %collective-permute-start = (bf16[512,128]{1,0:T(8,128)(2,1)S(1)}, bf16[512,128]{1,0:T(8,128)(2,1)S(1)}, u32[]{:S(2)}, u32[]{:S(2)}) collective-permute-start(bf16[512,128]{1,0:T(8,128)(2,1)S(1)} %join.1.refs_5_.refs_6_), channel_id=1, source_target_pairs={{0,4},{4,8},{8,12},{12,16},{16,20},{20,24},{24,28},{28,0},{1,5},{5... | collective-permute-start | bytes 393224 | tf_op jit(solution)/shard_map/ppermute | solution.py:17
  10.2 6.8 %collective-permute-start.3 = (bf16[512,128]{1,0:T(8,128)(2,1)S(1)}, bf16[512,128]{1,0:T(8,128)(2,1)S(1)}, u32[]{:S(2)}, u32[]{:S(2)}) collective-permute-start(bf16[512,128]{1,0:T(8,128)(2,1)S(1)} %collective-permute-done.1.refs_7_), channel_id=1, source_target_pairs={{0,8},{4,12},{8,16},{12,20},{16,24},{20,28},{24,0},{28,4},{1,9},{5... | collective-permute-start | bytes 393224 | tf_op jit(solution)/shard_map/ppermute | solution.py:17
  10.2 10.2 %collective-permute-start.2 = (bf16[512,128]{1,0:T(8,128)(2,1)S(1)}, bf16[512,128]{1,0:T(8,128)(2,1)S(1)}, u32[]{:S(2)}, u32[]{:S(2)}) collective-permute-start(bf16[512,128]{1,0:T(8,128)(2,1)S(1)} %collective-permute-done.1.refs_7_), channel_id=1, source_target_pairs={{0,4},{4,8},{8,12},{12,16},{16,20},{20,24},{24,28},{28,0},{1,5},{5... | collective-permute-start | bytes 393224 | tf_op jit(solution)/shard_map/ppermute | solution.py:17
  34.1 6.9 %collective-permute-start.4 = (bf16[2,256,256]{2,1,0:T(8,128)(2,1)S(1)}, bf16[2,256,256]{2,1,0:T(8,128)(2,1)S(1)}, u32[]{:S(2)}, u32[]{:S(2)}) collective-permute-start(bf16[2,256,256]{2,1,0:T(8,128)(2,1)S(1)} %get-tuple-element.33), channel_id=1, source_target_pairs={{0,24},{4,28},{8,0},{12,4},{16,8},{20,12},{24,16},{28,20},{1,25},{... | collective-permute-start | bytes 786440 | tf_op jit(solution)/shard_map/ppermute | solution.py:17
  41.0 6.2 %collective-permute-start.6 = (bf16[256,256]{1,0:T(8,128)(2,1)S(1)}, bf16[256,256]{1,0:T(8,128)(2,1)S(1)}, u32[]{:S(2)}, u32[]{:S(2)}) collective-permute-start(bf16[256,256]{1,0:T(8,128)(2,1)S(1)} %get-tuple-element.36), channel_id=1, source_target_pairs={{0,24},{4,28},{8,0},{12,4},{16,8},{20,12},{24,16},{28,20},{1,25},{... | collective-permute-start | bytes 393224 | tf_op jit(solution)/shard_map/ppermute | solution.py:17
  43.3 5.0 %collective-permute-start.5 = (bf16[256,256]{1,0:T(8,128)(2,1)S(1)}, bf16[256,256]{1,0:T(8,128)(2,1)S(1)}, u32[]{:S(2)}, u32[]{:S(2)}) collective-permute-start(bf16[256,256]{1,0:T(8,128)(2,1)S(1)} %get-tuple-element.37), channel_id=1, source_target_pairs={{0,28},{4,0},{8,4},{12,8},{16,12},{20,16},{24,20},{28,24},{1,29},{... | collective-permute-start | bytes 393224 | tf_op jit(solution)/shard_map/ppermute | solution.py:17

commit v3 on v2

--- a/solution.py
+++ b/solution.py
@@ -59,8 +59,8 @@
     return jnp.sum(left.astype(jnp.float32) * right.astype(jnp.float32), axis=1, keepdims=True)
 
 
-def backward_group(group, pack, width, g, delta, slots, q_t, g_t, weights, kv_refs, grad_ref):
-    tokens = kv_refs[0].shape[0] // 2
+def backward_group(g, delta, q_t, g_t, weights, kv_refs, grad_ref):
+    tokens, width = kv_refs[0].shape[0] // 2, kv_refs[0].shape[1]
     steps = []
     for index, (w, kv_ref) in enumerate(zip(weights, kv_refs)):
         dp = dot_nt(g, kv_ref[tokens:])
@@ -122,47 +122,86 @@
     values_ref[...] = total[width:].T.astype(jnp.bfloat16)
 
 
-def first_kernel(slot_count, near, pack, head_count, score_scale, *refs):
-    bias_ref, q_ref, qt_ref, g_ref, gt_ref = refs[:5]
-    kv_refs = refs[5 : 5 + slot_count]
-    out_ref, dq_ref, grad_out_ref, kept_ref, delta_ref, vext_ref, grad_ref = refs[5 + slot_count :]
+def forward_slots(q, bias_ref, first_slot, kv_refs, vext_ref, factor, pack, top):
+    rows = q.shape[0]
+    tokens = rows // pack
+    scores = []
+    for index, kv_ref in enumerate(kv_refs):
+        part = dot_nt(q, kv_ref[:tokens]).reshape(pack, tokens, tokens)
+        part = (part * factor + bias_ref[first_slot + index][None]).reshape(rows, tokens)
+        scores.append(part)
+    highest = scores[0]
+    for part in scores[1:]:
+        highest = jnp.maximum(highest, part)
+    highest = jnp.max(highest, axis=1, keepdims=True)
+    if top is not None:
+        highest = jnp.maximum(highest, top)
+    weights = [jnp.exp2(part - highest).astype(jnp.bfloat16) for part in scores]
+    total = split_chain(weights, [vext_ref[index] for index in range(len(kv_refs))], 2)
+    return highest, weights, total
+
+
+def extend_values(kv_refs, vext_ref):
+    tokens, width = kv_refs[0].shape[0] // 2, kv_refs[0].shape[1]
+    for index, kv_ref in enumerate(kv_refs):
+        vext_ref[index, :, :width] = kv_ref[tokens:]
+        vext_ref[index, :, width:] = jnp.ones((tokens, width), jnp.bfloat16)
+
+
+def near_kernel(slots, pack, head_count, score_scale, *refs):
+    bias_ref, q_ref = refs[:2]
+    kv_refs = refs[2 : 2 + slots]
+    kept_ref, total_ref, top_ref, vext_ref = refs[2 + slots :]
+    width = q_ref.shape[1] // head_count
+    rows = pack * q_ref.shape[0]
+    extend_values(kv_refs, vext_ref)
+
+    def one_group(group, carry):
+        q = take_rows(q_ref, group, pack, width)
+        top, weights, total = forward_slots(
+            q, bias_ref, 0, kv_refs, vext_ref, score_scale * LOG2_E, pack, None
+        )
+        group_rows = pl.ds(pl.multiple_of(group * rows, rows), rows)
+        for slot in range(slots):
+            kept_ref[slot, group_rows] = weights[slot]
+        total_ref[group_rows] = total
+        top_ref[group_rows] = jnp.broadcast_to(top, (rows, width))
+        return carry
+
+    lax.fori_loop(0, head_count // pack, one_group, 0)
+
+
+def far_kernel(first_slot, slots, pack, head_count, score_scale, *refs):
+    bias_ref, q_ref, qt_ref, g_ref, gt_ref, total_ref, top_ref = refs[:7]
+    kv_refs = refs[7 : 7 + slots]
+    out_ref, dq_ref, grad_out_ref, rate_ref, delta_ref, vext_ref, grad_ref = refs[7 + slots :]
     tokens = q_ref.shape[0]
     width = q_ref.shape[1] // head_count
     rows = pack * tokens
-    factor = score_scale * LOG2_E
-    for slot in range(slot_count):
-        vext_ref[slot, :, :width] = kv_refs[slot][tokens:]
-        vext_ref[slot, :, width:] = jnp.ones((tokens, width), jnp.bfloat16)
+    extend_values(kv_refs, vext_ref)
     grad_ref[...] = jnp.zeros(grad_ref.shape, jnp.float32)
 
     def one_group(group, carry):
+        group_rows = pl.ds(pl.multiple_of(group * rows, rows), rows)
         q = take_rows(q_ref, group, pack, width)
         g = take_rows(g_ref, group, pack, width)
-        scores = []
-        top = None
-        for slot in range(slot_count):
-            s = dot_nt(q, kv_refs[slot][:tokens]).reshape(pack, tokens, tokens)
-            s = (s * factor + bias_ref[slot][None]).reshape(rows, tokens)
-            scores.append(s)
-            top = s if top is None else jnp.maximum(top, s)
-        top = jnp.max(top, axis=1, keepdims=True)
-        weights = [jnp.exp2(s - top).astype(jnp.bfloat16) for s in scores]
-        total = split_chain(weights, [vext_ref[slot] for slot in range(slot_count)], 2)
-        inverse = 1.0 / total[:, width:]
-        out = (total[:, :width] * inverse).astype(jnp.bfloat16)
+        near_top = top_ref[group_rows]
+        top, weights, total = forward_slots(
+            q, bias_ref, first_slot, kv_refs, vext_ref, score_scale * LOG2_E, pack, near_top[:, :1]
+        )
+        shrink = jnp.exp2(near_top - top)
+        near_total = total_ref[group_rows]
+        inverse = 1.0 / (near_total[:, width:] * shrink + total[:, width:])
+        out = ((near_total[:, :width] * shrink + total[:, :width]) * inverse).astype(jnp.bfloat16)
         put_rows(out_ref, group, pack, width, out)
         delta = row_dots(g, out)
+        delta_ref[group_rows] = jnp.broadcast_to(delta, (rows, width))
+        rate_ref[group_rows] = shrink * inverse
         inverse = jnp.concatenate([inverse] * (tokens // width), axis=1)
         weights = [(w.astype(jnp.float32) * inverse).astype(jnp.bfloat16) for w in weights]
-        group_rows = pl.ds(pl.multiple_of(group * rows, rows), rows)
-        delta_ref[group_rows] = jnp.broadcast_to(delta, (rows, width))
-        for slot in range(near):
-            kept_ref[slot, group_rows] = weights[slot]
         q_t = take_columns(qt_ref, group, pack, width)
         g_t = take_columns(gt_ref, group, pack, width)
-        dq = backward_group(
-            group, pack, width, g, delta, slot_count, q_t, g_t, weights[near:], kv_refs[near:], grad_ref
-        )
+        dq = backward_group(g, delta, q_t, g_t, weights, kv_refs, grad_ref)
         put_rows(dq_ref, group, pack, width, dq)
         return carry
 
@@ -171,9 +210,9 @@
 
 
 def later_kernel(first_slot, slots, pack, head_count, dq_scale, *refs):
-    qt_ref, g_ref, gt_ref, delta_ref, kept_ref, dq_in_ref = refs[:6]
-    kv_refs = refs[6 : 6 + slots]
-    dq_ref, grad_ref = refs[6 + slots :]
+    qt_ref, g_ref, gt_ref, rate_ref, delta_ref, kept_ref, dq_in_ref = refs[:7]
+    kv_refs = refs[7 : 7 + slots]
+    dq_ref, grad_ref = refs[7 + slots :]
     tokens = g_ref.shape[0]
     width = g_ref.shape[1] // head_count
     rows = pack * tokens
@@ -183,12 +222,14 @@
         g = take_rows(g_ref, group, pack, width)
         group_rows = pl.ds(pl.multiple_of(group * rows, rows), rows)
         delta = jnp.concatenate([delta_ref[group_rows]] * (tokens // width), axis=1)
-        weights = [kept_ref[first_slot + index, group_rows] for index in range(slots)]
+        rate = jnp.concatenate([rate_ref[group_rows]] * (tokens // width), axis=1)
+        weights = [
+            (kept_ref[first_slot + index, group_rows].astype(jnp.float32) * rate).astype(jnp.bfloat16)
+            for index in range(slots)
+        ]
         q_t = take_columns(qt_ref, group, pack, width)
         g_t = take_columns(gt_ref, group, pack, width)
-        dq = backward_group(
-            group, pack, width, g, delta, slots, q_t, g_t, weights, kv_refs, grad_ref
-        )
+        dq = backward_group(g, delta, q_t, g_t, weights, kv_refs, grad_ref)
         dq = dq + take_rows(dq_in_ref, group, pack, width)
         put_rows(dq_ref, group, pack, width, (dq * dq_scale).astype(dq_ref.dtype))
         return carry
@@ -248,32 +289,52 @@
     )(own, *parts)
 
 
-def first_call(bias, q, qt, g, gt, kvs, near, pack, head_count, score_scale):
-    slot_count = len(kvs)
+def near_call(bias, q, kvs, pack, head_count, score_scale):
+    slots = len(kvs)
     tokens = q.shape[0]
     width = q.shape[1] // head_count
-    far = slot_count - near
-    return pl.pallas_call(
-        functools.partial(first_kernel, slot_count, near, pack, head_count, score_scale),
+    rows = head_count * tokens
+    return pl.pallas_call(
+        functools.partial(near_kernel, slots, pack, head_count, score_scale),
+        out_shape=(
+            jax.ShapeDtypeStruct((slots, rows, tokens), jnp.bfloat16),
+            jax.ShapeDtypeStruct((rows, 2 * width), jnp.float32),
+            jax.ShapeDtypeStruct((rows, width), jnp.float32),
+        ),
+        in_specs=[VMEM] * (2 + slots),
+        out_specs=(VMEM,) * 3,
+        scratch_shapes=[pltpu.VMEM((slots, tokens, 2 * width), jnp.bfloat16)],
+        compiler_params=pltpu.CompilerParams(vmem_limit_bytes=(slots + 1) * (4 << 20)),
+        name="forward_near",
+    )(bias, q, *kvs)
+
+
+def far_call(bias, q, qt, g, gt, total, top, kvs, first_slot, pack, head_count, score_scale):
+    slots = len(kvs)
+    tokens = q.shape[0]
+    width = q.shape[1] // head_count
+    rows = head_count * tokens
+    return pl.pallas_call(
+        functools.partial(far_kernel, first_slot, slots, pack, head_count, score_scale),
         out_shape=(
             jax.ShapeDtypeStruct(q.shape, jnp.bfloat16),
             jax.ShapeDtypeStruct(q.shape, jnp.float32),
-            jax.ShapeDtypeStruct((far, 2 * width, tokens), jnp.bfloat16),
-            jax.ShapeDtypeStruct((near, head_count * tokens, tokens), jnp.bfloat16),
-            jax.ShapeDtypeStruct((head_count * tokens, width), jnp.float32),
+            jax.ShapeDtypeStruct((slots, 2 * width, tokens), jnp.bfloat16),
+            jax.ShapeDtypeStruct((rows, width), jnp.float32),
+            jax.ShapeDtypeStruct((rows, width), jnp.float32),
         ),
-        in_specs=[VMEM] * (5 + slot_count),
+        in_specs=[VMEM] * (7 + slots),
         out_specs=(VMEM,) * 5,
         scratch_shapes=[
-            pltpu.VMEM((slot_count, tokens, 2 * width), jnp.bfloat16),
-            pltpu.VMEM((far, 2 * width, tokens), jnp.float32),
+            pltpu.VMEM((slots, tokens, 2 * width), jnp.bfloat16),
+            pltpu.VMEM((slots, 2 * width, tokens), jnp.float32),
         ],
-        compiler_params=pltpu.CompilerParams(vmem_limit_bytes=slot_count * (5 << 20)),
+        compiler_params=pltpu.CompilerParams(vmem_limit_bytes=(slots + 1) * (5 << 20)),
         name="forward_far",
-    )(bias, q, qt, g, gt, *kvs)
-
-
-def later_call(qt, g, gt, delta, kept, dq, kvs, first_slot, pack, head_count, dq_scale, last):
+    )(bias, q, qt, g, gt, total, top, *kvs)
+
+
+def later_call(qt, g, gt, rate, delta, kept, dq, kvs, first_slot, pack, head_count, dq_scale, last):
     slots = len(kvs)
     tokens = g.shape[0]
     width = g.shape[1] // head_count
@@ -283,11 +344,11 @@
             jax.ShapeDtypeStruct(g.shape, jnp.bfloat16 if last else jnp.float32),
             jax.ShapeDtypeStruct((slots, 2 * width, tokens), jnp.float32),
         ),
-        in_specs=[VMEM] * (6 + slots),
+        in_specs=[VMEM] * (7 + slots),
         out_specs=(VMEM,) * 2,
         compiler_params=pltpu.CompilerParams(vmem_limit_bytes=slots * (3 << 20)),
         name="backward_near",
-    )(qt, g, gt, delta, kept, dq, *kvs)
+    )(qt, g, gt, rate, delta, kept, dq, *kvs)
 
 
 def shards(queries, keys, values, lengths, grad_out):
@@ -297,33 +358,29 @@
     score_scale = 1.0 / math.sqrt(width)
     pack = math.gcd(8, head_count)
 
+    near = reach // 2 + 1
     own = join_call(keys, values)
-    window = [own]
-    if reach > 1:
-        two = ring_shift(own, 2)
-        one = ring_shift(own, 1)
-        window += [one, two]
-    else:
-        window += [ring_shift(own, 1)]
+    two = ring_shift(own, 2)
+    one = ring_shift(own, 1)
+    queries, grad_out, queries_t, grads_t, bias = prepare_call(
+        lengths, queries, grad_out, reach + 1
+    )
+    two, bias = lax.optimization_barrier((two, bias))
+    window = [own, one, two]
     if reach > 2:
-        four = ring_shift(two, 2)
-        three = ring_shift(two, 1)
-        window += [three, four]
+        window += [ring_shift(two, 1), ring_shift(two, 2)]
     while len(window) <= reach:
         shift = len(window) - 1
         window += [ring_shift(part, shift) for part in window[1:]]
-
-    queries, grad_out, queries_t, grads_t, bias = prepare_call(
-        lengths, queries, grad_out, reach + 1
-    )
-
-    near = reach // 2 + 1
-    out, dq, far_grads, kept, delta = first_call(
-        bias, queries, queries_t, grad_out, grads_t, window, near, pack, head_count, score_scale
+    window = window[: reach + 1]
+
+    kept, total, top = near_call(bias, queries, window[:near], pack, head_count, score_scale)
+    out, dq, far_grads, rate, delta = far_call(
+        bias, queries, queries_t, grad_out, grads_t, total, top, window[near:], near, pack, head_count, score_scale
     )
     moved = ring_shift(far_grads, -(reach // 2))
     dq, near_grads = later_call(
-        queries_t, grad_out, grads_t, delta, kept, dq, window[1:near], 1, pack, head_count, 1.0, False
+        queries_t, grad_out, grads_t, rate, delta, kept, dq, window[1:near], 1, pack, head_count, 1.0, False
     )
     near_grads = (near_grads + moved.astype(jnp.float32)).astype(jnp.bfloat16)
     while near_grads.shape[0] > 2:
@@ -332,7 +389,7 @@
         near_grads = (near_grads[:half].astype(jnp.float32) + back.astype(jnp.float32)).astype(jnp.bfloat16)
     received = [ring_shift(near_grads[i], -1 - i) for i in range(near_grads.shape[0])]
     dq, own_grads = later_call(
-        queries_t, grad_out, grads_t, delta, kept, dq, window[:1], 0, pack, head_count, score_scale, True
+        queries_t, grad_out, grads_t, rate, delta, kept, dq, window[:1], 0, pack, head_count, score_scale, True
     )
     grad_keys, grad_values = finish_call(own_grads, received, score_scale, width)
     return (out, dq, grad_keys, grad_values)

time: 49.3 us -> 45.3 us (0.919)
  waiting for transfers between devices: 11.5 us -> 5.41 us
  starting transfers between devices: 10.4 us -> 12.1 us
  Pallas kernels: 26.3 us -> 26.9 us
    ppermute x7, waiting for transfers between devices: 11.5 us -> 5.41 us  [ring_shift(): lax.ppermute(value, 'seq', [(i, (i + steps) % count) for i in range(count)])]
    ppermute x7, starting transfers between devices: 10.4 us -> 12.1 us  [ring_shift(): lax.ppermute(value, 'seq', [(i, (i + steps) % count) for i in range(count)])]
    pallas_call x1 -> x2, Pallas kernels: 13.7 us -> 14.3 us  [the longest x1 9.24 us: far_call(): pl.pallas_call(functools.partial(far_kernel, first_slot, slots, pack, hea...]
  transfers between devices with their start and end apart: 7 -> 7, of which waited for: 5 -> 5; matrix products, arithmetic and copies ran while one was open for 0% -> 0% of each run, Pallas kernels for 22% -> 35%
where the time goes in v3:
time: 45.3 us; the launch traced here: 45.1 us
  Pallas kernels  26.9 us (59%)
  starting transfers between devices  12.1 us (27%)
  waiting for transfers between devices  5.41 us (12%)
  between operations  0.69 us (2%)
    ppermute x7, starting transfers between devices, ring_shift(): lax.ppermute(value, 'seq', [(i, (i + steps) % count) for i in range(count)])  12.1 us
    pallas_call x1, Pallas kernels, far_call(): pl.pallas_call(functools.partial(far_kernel, first_slot, slots, pack, hea...  9.24 us
    pallas_call x2, Pallas kernels, later_call(): pl.pallas_call(functools.partial(later_kernel, first_slot, slots, pack, h...  8.42 us
    ppermute x7, waiting for transfers between devices, ring_shift(): lax.ppermute(value, 'seq', [(i, (i + steps) % count) for i in range(count)])  5.41 us
    pallas_call x1, Pallas kernels, near_call(): pl.pallas_call(functools.partial(near_kernel, slots, pack, head_count, sc...  5.03 us
    pallas_call x1, Pallas kernels, prepare_call(): pl.pallas_call(functools.partial(prepare_kernel, slot_count), out_shape=(...  2.56 us
  transfers between devices with their start and end apart: 7, of which 5 were waited for; matrix products, arithmetic and copies ran while one was open for 0% of the time, Pallas kernels for 35%

profile of v3, /device:TPU:0, one launch (start us, length us, event | category | flops | bytes accessed | tf_op | source)
XLA Modules:
  0.0 45.1 jit_solution(14630138595239771768)
XLA Ops:
  0.6 0.9 %join.1.refs_2_.refs_7_ = bf16[512,128]{1,0:T(8,128)(2,1)S(1)} custom-call(bf16[256,128]{1,0:T(8,128)(2,1)} %keys_ref.1, bf16[256,128]{1,0:T(8,128)(2,1)} %values_ref.1), custom_call_target="tpu_custom_call" | custom-call | tf_op jit(solution)/shard_map/join/pallas_call | solution.py:249
  1.5 3.1 %collective-permute-start = (bf16[512,128]{1,0:T(8,128)(2,1)S(1)}, bf16[512,128]{1,0:T(8,128)(2,1)S(1)}, u32[]{:S(2)}, u32[]{:S(2)}) collective-permute-start(bf16[512,128]{1,0:T(8,128)(2,1)S(1)} %join.1.refs_2_.refs_7_), channel_id=1, source_target_pairs={{0,8},{4,12},{8,16},{12,20},{16,24},{20,28},{24,0},{28,4},{1,9},{5... | collective-permute-start | bytes 393224 | tf_op jit(solution)/shard_map/ppermute | solution.py:17
  4.6 1.5 %collective-permute-start.1 = (bf16[512,128]{1,0:T(8,128)(2,1)S(1)}, bf16[512,128]{1,0:T(8,128)(2,1)S(1)}, u32[]{:S(2)}, u32[]{:S(2)}) collective-permute-start(bf16[512,128]{1,0:T(8,128)(2,1)S(1)} %join.1.refs_2_.refs_7_), channel_id=1, source_target_pairs={{0,4},{4,8},{8,12},{12,16},{16,20},{20,24},{24,28},{28,0},{1,5},{5... | collective-permute-start | bytes 393224 | tf_op jit(solution)/shard_map/ppermute | solution.py:17
  6.2 2.6 %prepare.1 = (bf16[256,2048]{1,0:T(8,128)(2,1)S(1)}, bf16[256,2048]{1,0:T(8,128)(2,1)S(1)}, bf16[2048,256]{1,0:T(8,128)(2,1)S(1)}, bf16[2048,256]{1,0:T(8,128)(2,1)S(1)}, f32[5,256,256]{2,1,0:T(8,128)S(1)}) custom-call(s32[8]{0:T(128)} %lengths_ref.1, bf16[256,2048]{1,0:T(8,128)(2,1)} %q_in.1, bf16[256,2048]{1,0:T(8,128)(2,1)} %g_in.1), custom_call_target="tpu_custom_call" | custom-call | tf_op jit(solution)/shard_map/prepare/pallas_call | solution.py:262
  8.7 1.4 %collective-permute-done.refs_4_.refs_8_ = bf16[512,128]{1,0:T(8,128)(2,1)S(1)} collective-permute-done((bf16[512,128]{1,0:T(8,128)(2,1)S(1)}, bf16[512,128]{1,0:T(8,128)(2,1)S(1)}, u32[]{:S(2)}, u32[]{:S(2)}) %collective-permute-start) | collective-permute-done | bytes 131104 | tf_op jit(solution)/shard_map/ppermute | solution.py:17
  10.2 0.2 collective-permute-start.3
  10.4 2.4 %collective-permute-start.2 = (bf16[512,128]{1,0:T(8,128)(2,1)S(1)}, bf16[512,128]{1,0:T(8,128)(2,1)S(1)}, u32[]{:S(2)}, u32[]{:S(2)}) collective-permute-start(bf16[512,128]{1,0:T(8,128)(2,1)S(1)} %collective-permute-done.refs_4_.refs_8_), channel_id=1, source_target_pairs={{0,4},{4,8},{8,12},{12,16},{16,20},{20,24},{24,28},{28,0},{1,5},{5... | collective-permute-start | bytes 393224 | tf_op jit(solution)/shard_map/ppermute | solution.py:17
  12.7 1.2 %collective-permute-done.1.refs_3_.refs_7_ = bf16[512,128]{1,0:T(8,128)(2,1)S(1)} collective-permute-done((bf16[512,128]{1,0:T(8,128)(2,1)S(1)}, bf16[512,128]{1,0:T(8,128)(2,1)S(1)}, u32[]{:S(2)}, u32[]{:S(2)}) %collective-permute-start.1) | collective-permute-done | bytes 131104 | tf_op jit(solution)/shard_map/ppermute | solution.py:17
  13.9 5.0 %forward_near.1 = (bf16[3,4096,256]{2,1,0:T(8,128)(2,1)S(1)}, f32[4096,256]{1,0:T(8,128)S(1)}, f32[4096,128]{1,0:T(8,128)S(1)}) custom-call(f32[5,256,256]{2,1,0:T(8,128)S(1)} %get-tuple-element.26.refs_0_, bf16[256,2048]{1,0:T(8,128)(2,1)S(1)} %get-tuple-element.27.refs_1_, bf16[512,128]{1,0:T(8,128)(2,1)S(1)} %join.1.refs_2_.refs_7_, ...), custom_call_target="tpu_custom_call" | custom-call | tf_op jit(solution)/shard_map/forward_near/pallas_call | solution.py:297
  19.0 0.0 collective-permute-done.3.refs_8_
  19.0 1.4 %collective-permute-done.2.refs_7_ = bf16[512,128]{1,0:T(8,128)(2,1)S(1)} collective-permute-done((bf16[512,128]{1,0:T(8,128)(2,1)S(1)}, bf16[512,128]{1,0:T(8,128)(2,1)S(1)}, u32[]{:S(2)}, u32[]{:S(2)}) %collective-permute-start.2) | collective-permute-done | bytes 131104 | tf_op jit(solution)/shard_map/ppermute | solution.py:17
  20.4 9.2 %forward_far.1 = (bf16[256,2048]{1,0:T(8,128)(2,1)}, f32[256,2048]{1,0:T(8,128)S(1)}, bf16[2,256,256]{2,1,0:T(8,128)(2,1)S(1)}, f32[4096,128]{1,0:T(8,128)S(1)}, f32[4096,128]{1,0:T(8,128)S(1)}) custom-call(f32[5,256,256]{2,1,0:T(8,128)S(1)} %get-tuple-element.26.refs_0_, bf16[256,2048]{1,0:T(8,128)(2,1)S(1)} %get-tuple-element.27.refs_1_, ...), custom_call_target="tpu_custom_call" | custom-call | tf_op jit(solution)/shard_map/forward_far/pallas_call | solution.py:317
  29.6 1.5 %collective-permute-start.4 = (bf16[2,256,256]{2,1,0:T(8,128)(2,1)S(1)}, bf16[2,256,256]{2,1,0:T(8,128)(2,1)S(1)}, u32[]{:S(2)}, u32[]{:S(2)}) collective-permute-start(bf16[2,256,256]{2,1,0:T(8,128)(2,1)S(1)} %get-tuple-element.43), channel_id=1, source_target_pairs={{0,24},{4,28},{8,0},{12,4},{16,8},{20,12},{24,16},{28,20},{1,25},{... | collective-permute-start | bytes 786440 | tf_op jit(solution)/shard_map/ppermute | solution.py:17
  31.1 4.6 %backward_near.2 = (f32[256,2048]{1,0:T(8,128)S(1)}, f32[2,256,256]{2,1,0:T(8,128)S(1)}) custom-call(bf16[2048,256]{1,0:T(8,128)(2,1)S(1)} %get-tuple-element.28.refs_2_.refs_0_, bf16[256,2048]{1,0:T(8,128)(2,1)S(1)} %get-tuple-element.29.refs_3_.refs_1_, bf16[2048,256]{1,0:T(8,128)(2,1)S(1)} %get-tuple-element.30.refs_4_.refs_2_, ...), custom_call_target="tpu_custom_call" | custom-call | tf_op jit(solution)/shard_map/backward_near/pallas_call | solution.py:341
  35.7 0.3 collective-permute-done.4
  36.0 0.1 add_convert_fusion
  36.1 3.4 %collective-permute-start.6 = (bf16[256,256]{1,0:T(8,128)(2,1)S(1)}, bf16[256,256]{1,0:T(8,128)(2,1)S(1)}, u32[]{:S(2)}, u32[]{:S(2)}) collective-permute-start(bf16[256,256]{1,0:T(8,128)(2,1)S(1)} %get-tuple-element.46), channel_id=1, source_target_pairs={{0,24},{4,28},{8,0},{12,4},{16,8},{20,12},{24,16},{28,20},{1,25},{... | collective-permute-start | bytes 393224 | tf_op jit(solution)/shard_map/ppermute | solution.py:17
  39.4 0.0 collective-permute-start.5
  39.4 3.9 %backward_near.3 = (bf16[256,2048]{1,0:T(8,128)(2,1)}, f32[1,256,256]{2,1,0:T(8,128)S(1)}) custom-call(bf16[2048,256]{1,0:T(8,128)(2,1)S(1)} %get-tuple-element.28.refs_2_.refs_0_, bf16[256,2048]{1,0:T(8,128)(2,1)S(1)} %get-tuple-element.29.refs_3_.refs_1_, bf16[2048,256]{1,0:T(8,128)(2,1)S(1)} %get-tuple-element.30.refs_4_.refs_2_, ...), custom_call_target="tpu_custom_call" | custom-call | tf_op jit(solution)/shard_map/backward_near/pallas_call | solution.py:341
  43.3 0.0 collective-permute-done.6.refs_1_
  43.3 1.1 %collective-permute-done.5.refs_0_ = bf16[256,256]{1,0:T(8,128)(2,1)S(1)} collective-permute-done((bf16[256,256]{1,0:T(8,128)(2,1)S(1)}, bf16[256,256]{1,0:T(8,128)(2,1)S(1)}, u32[]{:S(2)}, u32[]{:S(2)}) %collective-permute-start.5) | collective-permute-done | bytes 131104 | tf_op jit(solution)/shard_map/ppermute | solution.py:17
  44.4 0.8 %finish.1 = (bf16[256,128]{1,0:T(8,128)(2,1)}, bf16[256,128]{1,0:T(8,128)(2,1)}) custom-call(f32[1,256,256]{2,1,0:T(8,128)S(1)} %get-tuple-element.41.own_ref, bf16[256,256]{1,0:T(8,128)(2,1)S(1)} %collective-permute-done.5.refs_0_, bf16[256,256]{1,0:T(8,128)(2,1)S(1)} %collective-permute-done.6.refs_1_), custom_call_target="tpu_custom_call" | custom-call | tf_op jit(solution)/shard_map/finish/pallas_call | solution.py:282
  (1 shorter events, 0.0 us)
Async XLA Ops:
  1.5 8.6 %collective-permute-start = (bf16[512,128]{1,0:T(8,128)(2,1)S(1)}, bf16[512,128]{1,0:T(8,128)(2,1)S(1)}, u32[]{:S(2)}, u32[]{:S(2)}) collective-permute-start(bf16[512,128]{1,0:T(8,128)(2,1)S(1)} %join.1.refs_2_.refs_7_), channel_id=1, source_target_pairs={{0,8},{4,12},{8,16},{12,20},{16,24},{20,28},{24,0},{28,4},{1,9},{5... | collective-permute-start | bytes 393224 | tf_op jit(solution)/shard_map/ppermute | solution.py:17
  4.6 9.3 %collective-permute-start.1 = (bf16[512,128]{1,0:T(8,128)(2,1)S(1)}, bf16[512,128]{1,0:T(8,128)(2,1)S(1)}, u32[]{:S(2)}, u32[]{:S(2)}) collective-permute-start(bf16[512,128]{1,0:T(8,128)(2,1)S(1)} %join.1.refs_2_.refs_7_), channel_id=1, source_target_pairs={{0,4},{4,8},{8,12},{12,16},{16,20},{20,24},{24,28},{28,0},{1,5},{5... | collective-permute-start | bytes 393224 | tf_op jit(solution)/shard_map/ppermute | solution.py:17
  10.2 8.8 %collective-permute-start.3 = (bf16[512,128]{1,0:T(8,128)(2,1)S(1)}, bf16[512,128]{1,0:T(8,128)(2,1)S(1)}, u32[]{:S(2)}, u32[]{:S(2)}) collective-permute-start(bf16[512,128]{1,0:T(8,128)(2,1)S(1)} %collective-permute-done.refs_4_.refs_8_), channel_id=1, source_target_pairs={{0,8},{4,12},{8,16},{12,20},{16,24},{20,28},{24,0},{28,4},{1,9},{5... | collective-permute-start | bytes 393224 | tf_op jit(solution)/shard_map/ppermute | solution.py:17
  10.4 10.0 %collective-permute-start.2 = (bf16[512,128]{1,0:T(8,128)(2,1)S(1)}, bf16[512,128]{1,0:T(8,128)(2,1)S(1)}, u32[]{:S(2)}, u32[]{:S(2)}) collective-permute-start(bf16[512,128]{1,0:T(8,128)(2,1)S(1)} %collective-permute-done.refs_4_.refs_8_), channel_id=1, source_target_pairs={{0,4},{4,8},{8,12},{12,16},{16,20},{20,24},{24,28},{28,0},{1,5},{5... | collective-permute-start | bytes 393224 | tf_op jit(solution)/shard_map/ppermute | solution.py:17
  29.6 6.4 %collective-permute-start.4 = (bf16[2,256,256]{2,1,0:T(8,128)(2,1)S(1)}, bf16[2,256,256]{2,1,0:T(8,128)(2,1)S(1)}, u32[]{:S(2)}, u32[]{:S(2)}) collective-permute-start(bf16[2,256,256]{2,1,0:T(8,128)(2,1)S(1)} %get-tuple-element.43), channel_id=1, source_target_pairs={{0,24},{4,28},{8,0},{12,4},{16,8},{20,12},{24,16},{28,20},{1,25},{... | collective-permute-start | bytes 786440 | tf_op jit(solution)/shard_map/ppermute | solution.py:17
  36.1 7.2 %collective-permute-start.6 = (bf16[256,256]{1,0:T(8,128)(2,1)S(1)}, bf16[256,256]{1,0:T(8,128)(2,1)S(1)}, u32[]{:S(2)}, u32[]{:S(2)}) collective-permute-start(bf16[256,256]{1,0:T(8,128)(2,1)S(1)} %get-tuple-element.46), channel_id=1, source_target_pairs={{0,24},{4,28},{8,0},{12,4},{16,8},{20,12},{24,16},{28,20},{1,25},{... | collective-permute-start | bytes 393224 | tf_op jit(solution)/shard_map/ppermute | solution.py:17
  39.4 5.0 %collective-permute-start.5 = (bf16[256,256]{1,0:T(8,128)(2,1)S(1)}, bf16[256,256]{1,0:T(8,128)(2,1)S(1)}, u32[]{:S(2)}, u32[]{:S(2)}) collective-permute-start(bf16[256,256]{1,0:T(8,128)(2,1)S(1)} %get-tuple-element.47), channel_id=1, source_target_pairs={{0,28},{4,0},{8,4},{12,8},{16,12},{20,16},{24,20},{28,24},{1,29},{... | collective-permute-start | bytes 393224 | tf_op jit(solution)/shard_map/ppermute | solution.py:17

commit v4 on v3

--- a/solution.py
+++ b/solution.py
@@ -55,20 +55,25 @@
     return jnp.concatenate(sums, axis=0)
 
 
+def split_nt(left, right, parts):
+    step = left.shape[0] // parts
+    return jnp.concatenate([dot_nt(left[i * step : (i + 1) * step], right) for i in range(parts)], axis=0)
+
+
 def row_dots(left, right):
     return jnp.sum(left.astype(jnp.float32) * right.astype(jnp.float32), axis=1, keepdims=True)
 
 
-def backward_group(g, delta, q_t, g_t, weights, kv_refs, grad_ref):
+def backward_slots(g, delta, q_t, g_t, weights, kv_refs, grad_ref, parts):
     tokens, width = kv_refs[0].shape[0] // 2, kv_refs[0].shape[1]
     steps = []
     for index, (w, kv_ref) in enumerate(zip(weights, kv_refs)):
-        dp = dot_nt(g, kv_ref[tokens:])
+        dp = split_nt(g, kv_ref[tokens:], parts)
         ds = (w.astype(jnp.float32) * (dp - delta)).astype(jnp.bfloat16)
         steps.append(ds)
         grad_ref[index, :width] += dot_nn(q_t, ds)
         grad_ref[index, width:] += dot_nn(g_t, w)
-    return split_chain(steps, [kv_ref[:tokens] for kv_ref in kv_refs], 2)
+    return steps
 
 
 def join_kernel(keys_ref, values_ref, own_ref, sems):
@@ -133,10 +138,11 @@
     highest = scores[0]
     for part in scores[1:]:
         highest = jnp.maximum(highest, part)
-    highest = jnp.max(highest, axis=1, keepdims=True)
+    highest = jnp.broadcast_to(jnp.max(highest, axis=1, keepdims=True), (rows, q.shape[1]))
     if top is not None:
         highest = jnp.maximum(highest, top)
-    weights = [jnp.exp2(part - highest).astype(jnp.bfloat16) for part in scores]
+    level = jnp.concatenate([highest] * (tokens // q.shape[1]), axis=1)
+    weights = [jnp.exp2(part - level).astype(jnp.bfloat16) for part in scores]
     total = split_chain(weights, [vext_ref[index] for index in range(len(kv_refs))], 2)
     return highest, weights, total
 
@@ -165,7 +171,7 @@
         for slot in range(slots):
             kept_ref[slot, group_rows] = weights[slot]
         total_ref[group_rows] = total
-        top_ref[group_rows] = jnp.broadcast_to(top, (rows, width))
+        top_ref[group_rows] = top
         return carry
 
     lax.fori_loop(0, head_count // pack, one_group, 0)
@@ -174,7 +180,7 @@
 def far_kernel(first_slot, slots, pack, head_count, score_scale, *refs):
     bias_ref, q_ref, qt_ref, g_ref, gt_ref, total_ref, top_ref = refs[:7]
     kv_refs = refs[7 : 7 + slots]
-    out_ref, dq_ref, grad_out_ref, rate_ref, delta_ref, vext_ref, grad_ref = refs[7 + slots :]
+    out_ref, step_ref, grad_out_ref, rate_ref, delta_ref, vext_ref, grad_ref = refs[7 + slots :]
     tokens = q_ref.shape[0]
     width = q_ref.shape[1] // head_count
     rows = pack * tokens
@@ -187,7 +193,7 @@
         g = take_rows(g_ref, group, pack, width)
         near_top = top_ref[group_rows]
         top, weights, total = forward_slots(
-            q, bias_ref, first_slot, kv_refs, vext_ref, score_scale * LOG2_E, pack, near_top[:, :1]
+            q, bias_ref, first_slot, kv_refs, vext_ref, score_scale * LOG2_E, pack, near_top
         )
         shrink = jnp.exp2(near_top - top)
         near_total = total_ref[group_rows]
@@ -201,18 +207,25 @@
         weights = [(w.astype(jnp.float32) * inverse).astype(jnp.bfloat16) for w in weights]
         q_t = take_columns(qt_ref, group, pack, width)
         g_t = take_columns(gt_ref, group, pack, width)
-        dq = backward_group(g, delta, q_t, g_t, weights, kv_refs, grad_ref)
-        put_rows(dq_ref, group, pack, width, dq)
+        steps = backward_slots(g, delta, q_t, g_t, weights, kv_refs, grad_ref, 1)
+        for slot in range(slots):
+            step_ref[slot, group_rows] = steps[slot]
         return carry
 
-    lax.fori_loop(0, head_count // pack, one_group, 0)
+    lax.fori_loop(0, head_count // pack, one_group, 0, unroll=True)
     grad_out_ref[...] = grad_ref[...].astype(grad_out_ref.dtype)
 
 
-def later_kernel(first_slot, slots, pack, head_count, dq_scale, *refs):
-    qt_ref, g_ref, gt_ref, rate_ref, delta_ref, kept_ref, dq_in_ref = refs[:7]
-    kv_refs = refs[7 : 7 + slots]
-    dq_ref, grad_ref = refs[7 + slots :]
+def later_kernel(first_slot, slots, pack, head_count, score_scale, *refs):
+    qt_ref, g_ref, gt_ref, rate_ref, delta_ref, kept_ref = refs[:6]
+    kv_refs = refs[6 : 6 + slots]
+    last = first_slot == 0
+    if last:
+        step_refs = refs[6 + slots : 8 + slots]
+        more_refs = refs[8 + slots : -2]
+        dq_ref, grad_ref = refs[-2:]
+    else:
+        step_ref, grad_ref = refs[6 + slots :]
     tokens = g_ref.shape[0]
     width = g_ref.shape[1] // head_count
     rows = pack * tokens
@@ -229,9 +242,15 @@
         ]
         q_t = take_columns(qt_ref, group, pack, width)
         g_t = take_columns(gt_ref, group, pack, width)
-        dq = backward_group(g, delta, q_t, g_t, weights, kv_refs, grad_ref)
-        dq = dq + take_rows(dq_in_ref, group, pack, width)
-        put_rows(dq_ref, group, pack, width, (dq * dq_scale).astype(dq_ref.dtype))
+        steps = backward_slots(g, delta, q_t, g_t, weights, kv_refs, grad_ref, 2)
+        if last:
+            for held_ref in step_refs:
+                steps = steps + [held_ref[slot, group_rows] for slot in range(held_ref.shape[0])]
+            dq = split_chain(steps, [ref[:tokens] for ref in (*kv_refs, *more_refs)], 2)
+            put_rows(dq_ref, group, pack, width, (dq * score_scale).astype(jnp.bfloat16))
+        else:
+            for slot in range(slots):
+                step_ref[slot, group_rows] = steps[slot]
         return carry
 
     lax.fori_loop(0, head_count // pack, one_group, 0)
@@ -318,7 +337,7 @@
         functools.partial(far_kernel, first_slot, slots, pack, head_count, score_scale),
         out_shape=(
             jax.ShapeDtypeStruct(q.shape, jnp.bfloat16),
-            jax.ShapeDtypeStruct(q.shape, jnp.float32),
+            jax.ShapeDtypeStruct((slots, rows, tokens), jnp.bfloat16),
             jax.ShapeDtypeStruct((slots, 2 * width, tokens), jnp.bfloat16),
             jax.ShapeDtypeStruct((rows, width), jnp.float32),
             jax.ShapeDtypeStruct((rows, width), jnp.float32),
@@ -329,26 +348,27 @@
             pltpu.VMEM((slots, tokens, 2 * width), jnp.bfloat16),
             pltpu.VMEM((slots, 2 * width, tokens), jnp.float32),
         ],
-        compiler_params=pltpu.CompilerParams(vmem_limit_bytes=(slots + 1) * (5 << 20)),
+        compiler_params=pltpu.CompilerParams(vmem_limit_bytes=(slots + 1) * (7 << 20)),
         name="forward_far",
     )(bias, q, qt, g, gt, total, top, *kvs)
 
 
-def later_call(qt, g, gt, rate, delta, kept, dq, kvs, first_slot, pack, head_count, dq_scale, last):
+def later_call(qt, g, gt, rate, delta, kept, kvs, steps, more, first_slot, pack, head_count, score_scale):
     slots = len(kvs)
     tokens = g.shape[0]
     width = g.shape[1] // head_count
-    return pl.pallas_call(
-        functools.partial(later_kernel, first_slot, slots, pack, head_count, dq_scale),
-        out_shape=(
-            jax.ShapeDtypeStruct(g.shape, jnp.bfloat16 if last else jnp.float32),
-            jax.ShapeDtypeStruct((slots, 2 * width, tokens), jnp.float32),
-        ),
-        in_specs=[VMEM] * (7 + slots),
+    if steps:
+        result = jax.ShapeDtypeStruct(g.shape, jnp.bfloat16)
+    else:
+        result = jax.ShapeDtypeStruct((slots, head_count * tokens, tokens), jnp.bfloat16)
+    return pl.pallas_call(
+        functools.partial(later_kernel, first_slot, slots, pack, head_count, score_scale),
+        out_shape=(result, jax.ShapeDtypeStruct((slots, 2 * width, tokens), jnp.float32)),
+        in_specs=[VMEM] * (6 + slots + len(steps) + len(more)),
         out_specs=(VMEM,) * 2,
-        compiler_params=pltpu.CompilerParams(vmem_limit_bytes=slots * (3 << 20)),
-        name="backward_near",
-    )(qt, g, gt, rate, delta, kept, dq, *kvs)
+        compiler_params=pltpu.CompilerParams(vmem_limit_bytes=(slots + 1) * (4 << 20)),
+        name="backward_last" if steps else "backward_near",
+    )(qt, g, gt, rate, delta, kept, *kvs, *steps, *more)
 
 
 def shards(queries, keys, values, lengths, grad_out):
@@ -356,7 +376,10 @@
     head_count = queries.shape[1] // width
     reach = min(8, lax.axis_size("seq") // 2)
     score_scale = 1.0 / math.sqrt(width)
-    pack = math.gcd(8, head_count)
+    pack_a = math.gcd(8, head_count)
+    pack_f = math.gcd(8, head_count)
+    pack_2 = math.gcd(16, head_count)
+    pack_3 = math.gcd(16, head_count)
 
     near = reach // 2 + 1
     own = join_call(keys, values)
@@ -374,13 +397,14 @@
         window += [ring_shift(part, shift) for part in window[1:]]
     window = window[: reach + 1]
 
-    kept, total, top = near_call(bias, queries, window[:near], pack, head_count, score_scale)
-    out, dq, far_grads, rate, delta = far_call(
-        bias, queries, queries_t, grad_out, grads_t, total, top, window[near:], near, pack, head_count, score_scale
+    kept, total, top = near_call(bias, queries, window[:near], pack_a, head_count, score_scale)
+    out, far_steps, far_grads, rate, delta = far_call(
+        bias, queries, queries_t, grad_out, grads_t, total, top, window[near:], near, pack_f, head_count, score_scale
     )
     moved = ring_shift(far_grads, -(reach // 2))
-    dq, near_grads = later_call(
-        queries_t, grad_out, grads_t, rate, delta, kept, dq, window[1:near], 1, pack, head_count, 1.0, False
+    shared = (queries_t, grad_out, grads_t, rate, delta, kept)
+    near_steps, near_grads = later_call(
+        *shared, window[1:near], [], [], 1, pack_2, head_count, score_scale
     )
     near_grads = (near_grads + moved.astype(jnp.float32)).astype(jnp.bfloat16)
     while near_grads.shape[0] > 2:
@@ -389,7 +413,7 @@
         near_grads = (near_grads[:half].astype(jnp.float32) + back.astype(jnp.float32)).astype(jnp.bfloat16)
     received = [ring_shift(near_grads[i], -1 - i) for i in range(near_grads.shape[0])]
     dq, own_grads = later_call(
-        queries_t, grad_out, grads_t, rate, delta, kept, dq, window[:1], 0, pack, head_count, score_scale, True
+        *shared, window[:1], [near_steps, far_steps], window[1:], 0, pack_3, head_count, score_scale
     )
     grad_keys, grad_values = finish_call(own_grads, received, score_scale, width)
     return (out, dq, grad_keys, grad_values)

time: 45.3 us -> 43.1 us (0.951)
  Pallas kernels: 26.9 us -> 23.8 us
  waiting for transfers between devices: 5.41 us -> 6.7 us
  starting transfers between devices: 12.1 us -> 11.6 us
    pallas_call x1, Pallas kernels: 9.24 us -> 6.46 us  [far_call(): pl.pallas_call(functools.partial(far_kernel, first_slot, slots, pack, hea...]
    ppermute x7, waiting for transfers between devices: 5.41 us -> 6.7 us  [ring_shift(): lax.ppermute(value, 'seq', [(i, (i + steps) % count) for i in range(count)])]
    ppermute x7, starting transfers between devices: 12.1 us -> 11.6 us  [ring_shift(): lax.ppermute(value, 'seq', [(i, (i + steps) % count) for i in range(count)])]
  transfers between devices with their start and end apart: 7 -> 7, of which waited for: 5 -> 4; matrix products, arithmetic and copies ran while one was open for 0% -> 0% of each run, Pallas kernels for 35% -> 37%
where the time goes in v4:
time: 43.1 us; the launch traced here: 42.9 us
  Pallas kernels  23.8 us (55%)
  starting transfers between devices  11.6 us (27%)
  waiting for transfers between devices  6.7 us (16%)
  between operations  0.69 us (2%)
    ppermute x7, starting transfers between devices, ring_shift(): lax.ppermute(value, 'seq', [(i, (i + steps) % count) for i in range(count)])  11.6 us
    pallas_call x2, Pallas kernels, later_call(): pl.pallas_call(functools.partial(later_kernel, first_slot, slots, pack, h...  8.14 us
    ppermute x7, waiting for transfers between devices, ring_shift(): lax.ppermute(value, 'seq', [(i, (i + steps) % count) for i in range(count)])  6.7 us
    pallas_call x1, Pallas kernels, far_call(): pl.pallas_call(functools.partial(far_kernel, first_slot, slots, pack, hea...  6.46 us
    pallas_call x1, Pallas kernels, near_call(): pl.pallas_call(functools.partial(near_kernel, slots, pack, head_count, sc...  5.03 us
    pallas_call x1, Pallas kernels, prepare_call(): pl.pallas_call(functools.partial(prepare_kernel, slot_count), out_shape=(...  2.56 us
    pallas_call x1, Pallas kernels, join_call(): pl.pallas_call(join_kernel, out_shape=jax.ShapeDtypeStruct((2 * keys.shap...  0.89 us
  transfers between devices with their start and end apart: 7, of which 4 were waited for; matrix products, arithmetic and copies ran while one was open for 0% of the time, Pallas kernels for 37%

profile of v4, /device:TPU:0, one launch (start us, length us, event | category | flops | bytes accessed | tf_op | source)
XLA Modules:
  0.0 42.9 jit_solution(5546591100648842833)
XLA Ops:
  0.6 0.9 %join.1.refs_2_.refs_6_ = bf16[512,128]{1,0:T(8,128)(2,1)S(1)} custom-call(bf16[256,128]{1,0:T(8,128)(2,1)} %keys_ref.1, bf16[256,128]{1,0:T(8,128)(2,1)} %values_ref.1), custom_call_target="tpu_custom_call" | custom-call | tf_op jit(solution)/shard_map/join/pallas_call | solution.py:268
  1.5 3.1 %collective-permute-start = (bf16[512,128]{1,0:T(8,128)(2,1)S(1)}, bf16[512,128]{1,0:T(8,128)(2,1)S(1)}, u32[]{:S(2)}, u32[]{:S(2)}) collective-permute-start(bf16[512,128]{1,0:T(8,128)(2,1)S(1)} %join.1.refs_2_.refs_6_), channel_id=1, source_target_pairs={{0,8},{4,12},{8,16},{12,20},{16,24},{20,28},{24,0},{28,4},{1,9},{5... | collective-permute-start | bytes 393224 | tf_op jit(solution)/shard_map/ppermute | solution.py:17
  4.6 1.5 %collective-permute-start.1 = (bf16[512,128]{1,0:T(8,128)(2,1)S(1)}, bf16[512,128]{1,0:T(8,128)(2,1)S(1)}, u32[]{:S(2)}, u32[]{:S(2)}) collective-permute-start(bf16[512,128]{1,0:T(8,128)(2,1)S(1)} %join.1.refs_2_.refs_6_), channel_id=1, source_target_pairs={{0,4},{4,8},{8,12},{12,16},{16,20},{20,24},{24,28},{28,0},{1,5},{5... | collective-permute-start | bytes 393224 | tf_op jit(solution)/shard_map/ppermute | solution.py:17
  6.2 2.6 %prepare.1 = (bf16[256,2048]{1,0:T(8,128)(2,1)S(1)}, bf16[256,2048]{1,0:T(8,128)(2,1)S(1)}, bf16[2048,256]{1,0:T(8,128)(2,1)S(1)}, bf16[2048,256]{1,0:T(8,128)(2,1)S(1)}, f32[5,256,256]{2,1,0:T(8,128)S(1)}) custom-call(s32[8]{0:T(128)} %lengths_ref.1, bf16[256,2048]{1,0:T(8,128)(2,1)} %q_in.1, bf16[256,2048]{1,0:T(8,128)(2,1)} %g_in.1), custom_call_target="tpu_custom_call" | custom-call | tf_op jit(solution)/shard_map/prepare/pallas_call | solution.py:281
  8.7 1.4 %collective-permute-done.refs_4_.refs_7_.refs_10_ = bf16[512,128]{1,0:T(8,128)(2,1)S(1)} collective-permute-done((bf16[512,128]{1,0:T(8,128)(2,1)S(1)}, bf16[512,128]{1,0:T(8,128)(2,1)S(1)}, u32[]{:S(2)}, u32[]{:S(2)}) %collective-permute-start) | collective-permute-done | bytes 131104 | tf_op jit(solution)/shard_map/ppermute | solution.py:17
  10.2 0.2 collective-permute-start.3
  10.4 2.4 %collective-permute-start.2 = (bf16[512,128]{1,0:T(8,128)(2,1)S(1)}, bf16[512,128]{1,0:T(8,128)(2,1)S(1)}, u32[]{:S(2)}, u32[]{:S(2)}) collective-permute-start(bf16[512,128]{1,0:T(8,128)(2,1)S(1)} %collective-permute-done.refs_4_.refs_7_.refs_10_), channel_id=1, source_target_pairs={{0,4},{4,8},{8,12},{12,16},{16,20},{20,24},{24,28},{28,0},{1,5},{5... | collective-permute-start | bytes 393224 | tf_op jit(solution)/shard_map/ppermute | solution.py:17
  12.7 1.2 %collective-permute-done.1.refs_3_.refs_6_.refs_9_ = bf16[512,128]{1,0:T(8,128)(2,1)S(1)} collective-permute-done((bf16[512,128]{1,0:T(8,128)(2,1)S(1)}, bf16[512,128]{1,0:T(8,128)(2,1)S(1)}, u32[]{:S(2)}, u32[]{:S(2)}) %collective-permute-start.1) | collective-permute-done | bytes 131104 | tf_op jit(solution)/shard_map/ppermute | solution.py:17
  13.9 5.0 %forward_near.1 = (bf16[3,4096,256]{2,1,0:T(8,128)(2,1)S(1)}, f32[4096,256]{1,0:T(8,128)S(1)}, f32[4096,128]{1,0:T(8,128)S(1)}) custom-call(f32[5,256,256]{2,1,0:T(8,128)S(1)} %get-tuple-element.26.refs_0_, bf16[256,2048]{1,0:T(8,128)(2,1)S(1)} %get-tuple-element.27.refs_1_, bf16[512,128]{1,0:T(8,128)(2,1)S(1)} %join.1.refs_2_.refs_6_, ...), custom_call_target="tpu_custom_call" | custom-call | tf_op jit(solution)/shard_map/forward_near/pallas_call | solution.py:316
  19.0 0.0 collective-permute-done.3.refs_8_.refs_12_
  19.0 1.4 %collective-permute-done.2.refs_7_.refs_11_ = bf16[512,128]{1,0:T(8,128)(2,1)S(1)} collective-permute-done((bf16[512,128]{1,0:T(8,128)(2,1)S(1)}, bf16[512,128]{1,0:T(8,128)(2,1)S(1)}, u32[]{:S(2)}, u32[]{:S(2)}) %collective-permute-start.2) | collective-permute-done | bytes 131104 | tf_op jit(solution)/shard_map/ppermute | solution.py:17
  20.4 6.5 %forward_far.1 = (bf16[256,2048]{1,0:T(8,128)(2,1)}, bf16[2,4096,256]{2,1,0:T(8,128)(2,1)S(1)}, bf16[2,256,256]{2,1,0:T(8,128)(2,1)S(1)}, f32[4096,128]{1,0:T(8,128)S(1)}, f32[4096,128]{1,0:T(8,128)S(1)}) custom-call(f32[5,256,256]{2,1,0:T(8,128)S(1)} %get-tuple-element.26.refs_0_, bf16[256,2048]{1,0:T(8,128)(2,1)S(1)} %get-tuple-element.27.refs_1_, ...), custom_call_target="tpu_custom_call" | custom-call | tf_op jit(solution)/shard_map/forward_far/pallas_call | solution.py:336
  26.8 1.7 %collective-permute-start.4 = (bf16[2,256,256]{2,1,0:T(8,128)(2,1)S(1)}, bf16[2,256,256]{2,1,0:T(8,128)(2,1)S(1)}, u32[]{:S(2)}, u32[]{:S(2)}) collective-permute-start(bf16[2,256,256]{2,1,0:T(8,128)(2,1)S(1)} %get-tuple-element.43), channel_id=1, source_target_pairs={{0,24},{4,28},{8,0},{12,4},{16,8},{20,12},{24,16},{28,20},{1,25},{... | collective-permute-start | bytes 786440 | tf_op jit(solution)/shard_map/ppermute | solution.py:17
  28.5 2.9 %backward_near.1 = (bf16[2,4096,256]{2,1,0:T(8,128)(2,1)S(1)}, f32[2,256,256]{2,1,0:T(8,128)S(1)}) custom-call(bf16[2048,256]{1,0:T(8,128)(2,1)S(1)} %get-tuple-element.28.refs_2_.refs_0_, bf16[256,2048]{1,0:T(8,128)(2,1)S(1)} %get-tuple-element.29.refs_3_.refs_1_, bf16[2048,256]{1,0:T(8,128)(2,1)S(1)} %get-tuple-element.30.refs_4_.refs_2_, ...), custom_call_target="tpu_custom_call" | custom-call | tf_op jit(solution)/shard_map/backward_near/pallas_call | solution.py:364
  31.5 2.7 %collective-permute-done.4 = bf16[2,256,256]{2,1,0:T(8,128)(2,1)S(1)} collective-permute-done((bf16[2,256,256]{2,1,0:T(8,128)(2,1)S(1)}, bf16[2,256,256]{2,1,0:T(8,128)(2,1)S(1)}, u32[]{:S(2)}, u32[]{:S(2)}) %collective-permute-start.4) | collective-permute-done | bytes 262176 | tf_op jit(solution)/shard_map/ppermute | solution.py:17
  34.2 0.1 add_convert_fusion
  34.3 2.6 %collective-permute-start.6 = (bf16[256,256]{1,0:T(8,128)(2,1)S(1)}, bf16[256,256]{1,0:T(8,128)(2,1)S(1)}, u32[]{:S(2)}, u32[]{:S(2)}) collective-permute-start(bf16[256,256]{1,0:T(8,128)(2,1)S(1)} %get-tuple-element.46), channel_id=1, source_target_pairs={{0,24},{4,28},{8,0},{12,4},{16,8},{20,12},{24,16},{28,20},{1,25},{... | collective-permute-start | bytes 393224 | tf_op jit(solution)/shard_map/ppermute | solution.py:17
  36.9 0.0 collective-permute-start.5
  36.9 5.2 %backward_last.1 = (bf16[256,2048]{1,0:T(8,128)(2,1)}, f32[1,256,256]{2,1,0:T(8,128)S(1)}) custom-call(bf16[2048,256]{1,0:T(8,128)(2,1)S(1)} %get-tuple-element.28.refs_2_.refs_0_, bf16[256,2048]{1,0:T(8,128)(2,1)S(1)} %get-tuple-element.29.refs_3_.refs_1_, bf16[2048,256]{1,0:T(8,128)(2,1)S(1)} %get-tuple-element.30.refs_4_.refs_2_, ...), custom_call_target="tpu_custom_call" | custom-call | tf_op jit(solution)/shard_map/backward_last/pallas_call | solution.py:364
  42.1 0.0 collective-permute-done.6.refs_1_
  42.1 0.0 collective-permute-done.5.refs_0_
  42.1 0.8 %finish.1 = (bf16[256,128]{1,0:T(8,128)(2,1)}, bf16[256,128]{1,0:T(8,128)(2,1)}) custom-call(f32[1,256,256]{2,1,0:T(8,128)S(1)} %get-tuple-element.41.own_ref, bf16[256,256]{1,0:T(8,128)(2,1)S(1)} %collective-permute-done.5.refs_0_, bf16[256,256]{1,0:T(8,128)(2,1)S(1)} %collective-permute-done.6.refs_1_), custom_call_target="tpu_custom_call" | custom-call | tf_op jit(solution)/shard_map/finish/pallas_call | solution.py:301
  (1 shorter events, 0.0 us)
Async XLA Ops:
  1.5 8.6 %collective-permute-start = (bf16[512,128]{1,0:T(8,128)(2,1)S(1)}, bf16[512,128]{1,0:T(8,128)(2,1)S(1)}, u32[]{:S(2)}, u32[]{:S(2)}) collective-permute-start(bf16[512,128]{1,0:T(8,128)(2,1)S(1)} %join.1.refs_2_.refs_6_), channel_id=1, source_target_pairs={{0,8},{4,12},{8,16},{12,20},{16,24},{20,28},{24,0},{28,4},{1,9},{5... | collective-permute-start | bytes 393224 | tf_op jit(solution)/shard_map/ppermute | solution.py:17
  4.6 9.3 %collective-permute-start.1 = (bf16[512,128]{1,0:T(8,128)(2,1)S(1)}, bf16[512,128]{1,0:T(8,128)(2,1)S(1)}, u32[]{:S(2)}, u32[]{:S(2)}) collective-permute-start(bf16[512,128]{1,0:T(8,128)(2,1)S(1)} %join.1.refs_2_.refs_6_), channel_id=1, source_target_pairs={{0,4},{4,8},{8,12},{12,16},{16,20},{20,24},{24,28},{28,0},{1,5},{5... | collective-permute-start | bytes 393224 | tf_op jit(solution)/shard_map/ppermute | solution.py:17
  10.2 8.8 %collective-permute-start.3 = (bf16[512,128]{1,0:T(8,128)(2,1)S(1)}, bf16[512,128]{1,0:T(8,128)(2,1)S(1)}, u32[]{:S(2)}, u32[]{:S(2)}) collective-permute-start(bf16[512,128]{1,0:T(8,128)(2,1)S(1)} %collective-permute-done.refs_4_.refs_7_.refs_10_), channel_id=1, source_target_pairs={{0,8},{4,12},{8,16},{12,20},{16,24},{20,28},{24,0},{28,4},{1,9},{5... | collective-permute-start | bytes 393224 | tf_op jit(solution)/shard_map/ppermute | solution.py:17
  10.4 10.0 %collective-permute-start.2 = (bf16[512,128]{1,0:T(8,128)(2,1)S(1)}, bf16[512,128]{1,0:T(8,128)(2,1)S(1)}, u32[]{:S(2)}, u32[]{:S(2)}) collective-permute-start(bf16[512,128]{1,0:T(8,128)(2,1)S(1)} %collective-permute-done.refs_4_.refs_7_.refs_10_), channel_id=1, source_target_pairs={{0,4},{4,8},{8,12},{12,16},{16,20},{20,24},{24,28},{28,0},{1,5},{5... | collective-permute-start | bytes 393224 | tf_op jit(solution)/shard_map/ppermute | solution.py:17
  26.8 7.4 %collective-permute-start.4 = (bf16[2,256,256]{2,1,0:T(8,128)(2,1)S(1)}, bf16[2,256,256]{2,1,0:T(8,128)(2,1)S(1)}, u32[]{:S(2)}, u32[]{:S(2)}) collective-permute-start(bf16[2,256,256]{2,1,0:T(8,128)(2,1)S(1)} %get-tuple-element.43), channel_id=1, source_target_pairs={{0,24},{4,28},{8,0},{12,4},{16,8},{20,12},{24,16},{28,20},{1,25},{... | collective-permute-start | bytes 786440 | tf_op jit(solution)/shard_map/ppermute | solution.py:17
  34.3 7.8 %collective-permute-start.6 = (bf16[256,256]{1,0:T(8,128)(2,1)S(1)}, bf16[256,256]{1,0:T(8,128)(2,1)S(1)}, u32[]{:S(2)}, u32[]{:S(2)}) collective-permute-start(bf16[256,256]{1,0:T(8,128)(2,1)S(1)} %get-tuple-element.46), channel_id=1, source_target_pairs={{0,24},{4,28},{8,0},{12,4},{16,8},{20,12},{24,16},{28,20},{1,25},{... | collective-permute-start | bytes 393224 | tf_op jit(solution)/shard_map/ppermute | solution.py:17
  36.9 5.2 %collective-permute-start.5 = (bf16[256,256]{1,0:T(8,128)(2,1)S(1)}, bf16[256,256]{1,0:T(8,128)(2,1)S(1)}, u32[]{:S(2)}, u32[]{:S(2)}) collective-permute-start(bf16[256,256]{1,0:T(8,128)(2,1)S(1)} %get-tuple-element.47), channel_id=1, source_target_pairs={{0,28},{4,0},{8,4},{12,8},{16,12},{20,16},{24,20},{28,24},{1,29},{... | collective-permute-start | bytes 393224 | tf_op jit(solution)/shard_map/ppermute | solution.py:17

commit v5 on v4

--- a/solution.py
+++ b/solution.py
@@ -220,12 +220,8 @@
     qt_ref, g_ref, gt_ref, rate_ref, delta_ref, kept_ref = refs[:6]
     kv_refs = refs[6 : 6 + slots]
     last = first_slot == 0
-    if last:
-        step_refs = refs[6 + slots : 8 + slots]
-        more_refs = refs[8 + slots : -2]
-        dq_ref, grad_ref = refs[-2:]
-    else:
-        step_ref, grad_ref = refs[6 + slots :]
+    carried_ref, more_refs = refs[6 + slots], refs[7 + slots : -2]
+    dq_ref, grad_ref = refs[-2:]
     tokens = g_ref.shape[0]
     width = g_ref.shape[1] // head_count
     rows = pack * tokens
@@ -243,14 +239,12 @@
         q_t = take_columns(qt_ref, group, pack, width)
         g_t = take_columns(gt_ref, group, pack, width)
         steps = backward_slots(g, delta, q_t, g_t, weights, kv_refs, grad_ref, 2)
+        if not last:
+            steps = steps + [carried_ref[slot, group_rows] for slot in range(carried_ref.shape[0])]
+        dq = split_chain(steps, [ref[:tokens] for ref in (*kv_refs, *more_refs)], 2)
         if last:
-            for held_ref in step_refs:
-                steps = steps + [held_ref[slot, group_rows] for slot in range(held_ref.shape[0])]
-            dq = split_chain(steps, [ref[:tokens] for ref in (*kv_refs, *more_refs)], 2)
-            put_rows(dq_ref, group, pack, width, (dq * score_scale).astype(jnp.bfloat16))
-        else:
-            for slot in range(slots):
-                step_ref[slot, group_rows] = steps[slot]
+            dq = (dq + take_rows(carried_ref, group, pack, width)) * score_scale
+        put_rows(dq_ref, group, pack, width, dq.astype(dq_ref.dtype))
         return carry
 
     lax.fori_loop(0, head_count // pack, one_group, 0)
@@ -353,22 +347,22 @@
     )(bias, q, qt, g, gt, total, top, *kvs)
 
 
-def later_call(qt, g, gt, rate, delta, kept, kvs, steps, more, first_slot, pack, head_count, score_scale):
+def later_call(qt, g, gt, rate, delta, kept, kvs, carried, more, first_slot, pack, head_count, score_scale):
     slots = len(kvs)
     tokens = g.shape[0]
     width = g.shape[1] // head_count
-    if steps:
-        result = jax.ShapeDtypeStruct(g.shape, jnp.bfloat16)
-    else:
-        result = jax.ShapeDtypeStruct((slots, head_count * tokens, tokens), jnp.bfloat16)
+    last = first_slot == 0
     return pl.pallas_call(
         functools.partial(later_kernel, first_slot, slots, pack, head_count, score_scale),
-        out_shape=(result, jax.ShapeDtypeStruct((slots, 2 * width, tokens), jnp.float32)),
-        in_specs=[VMEM] * (6 + slots + len(steps) + len(more)),
+        out_shape=(
+            jax.ShapeDtypeStruct(g.shape, jnp.bfloat16 if last else jnp.float32),
+            jax.ShapeDtypeStruct((slots, 2 * width, tokens), jnp.float32),
+        ),
+        in_specs=[VMEM] * (7 + slots + len(more)),
         out_specs=(VMEM,) * 2,
-        compiler_params=pltpu.CompilerParams(vmem_limit_bytes=(slots + 1) * (4 << 20)),
-        name="backward_last" if steps else "backward_near",
-    )(qt, g, gt, rate, delta, kept, *kvs, *steps, *more)
+        compiler_params=pltpu.CompilerParams(vmem_limit_bytes=(slots + len(more) + 1) * (4 << 20)),
+        name="backward_last" if last else "backward_near",
+    )(qt, g, gt, rate, delta, kept, *kvs, carried, *more)
 
 
 def shards(queries, keys, values, lengths, grad_out):
@@ -378,7 +372,7 @@
     score_scale = 1.0 / math.sqrt(width)
     pack_a = math.gcd(8, head_count)
     pack_f = math.gcd(8, head_count)
-    pack_2 = math.gcd(16, head_count)
+    pack_2 = math.gcd(8, head_count)
     pack_3 = math.gcd(16, head_count)
 
     near = reach // 2 + 1
@@ -403,8 +397,8 @@
     )
     moved = ring_shift(far_grads, -(reach // 2))
     shared = (queries_t, grad_out, grads_t, rate, delta, kept)
-    near_steps, near_grads = later_call(
-        *shared, window[1:near], [], [], 1, pack_2, head_count, score_scale
+    dq, near_grads = later_call(
+        *shared, window[1:near], far_steps, window[near:], 1, pack_2, head_count, score_scale
     )
     near_grads = (near_grads + moved.astype(jnp.float32)).astype(jnp.bfloat16)
     while near_grads.shape[0] > 2:
@@ -413,7 +407,7 @@
         near_grads = (near_grads[:half].astype(jnp.float32) + back.astype(jnp.float32)).astype(jnp.bfloat16)
     received = [ring_shift(near_grads[i], -1 - i) for i in range(near_grads.shape[0])]
     dq, own_grads = later_call(
-        *shared, window[:1], [near_steps, far_steps], window[1:], 0, pack_3, head_count, score_scale
+        *shared, window[:1], dq, [], 0, pack_3, head_count, score_scale
     )
     grad_keys, grad_values = finish_call(own_grads, received, score_scale, width)
     return (out, dq, grad_keys, grad_values)

time: 43.1 us -> 42.8 us (level)
  waiting for transfers between devices: 6.7 us -> 5.94 us
    ppermute x7, waiting for transfers between devices: 6.7 us -> 5.94 us  [ring_shift(): lax.ppermute(value, 'seq', [(i, (i + steps) % count) for i in range(count)])]
where the time goes in v5:
time: 42.8 us; the launch traced here: 42.6 us
  Pallas kernels  23.9 us (56%)
  starting transfers between devices  11.9 us (28%)
  waiting for transfers between devices  5.94 us (14%)
  between operations  0.71 us (2%)
    ppermute x7, starting transfers between devices, ring_shift(): lax.ppermute(value, 'seq', [(i, (i + steps) % count) for i in range(count)])  11.9 us
    pallas_call x2, Pallas kernels, later_call(): pl.pallas_call(functools.partial(later_kernel, first_slot, slots, pack, h...  8.22 us
    pallas_call x1, Pallas kernels, far_call(): pl.pallas_call(functools.partial(far_kernel, first_slot, slots, pack, hea...  6.46 us
    ppermute x7, waiting for transfers between devices, ring_shift(): lax.ppermute(value, 'seq', [(i, (i + steps) % count) for i in range(count)])  5.94 us
    pallas_call x1, Pallas kernels, near_call(): pl.pallas_call(functools.partial(near_kernel, slots, pack, head_count, sc...  5.03 us
    pallas_call x1, Pallas kernels, prepare_call(): pl.pallas_call(functools.partial(prepare_kernel, slot_count), out_shape=(...  2.56 us
    pallas_call x1, Pallas kernels, join_call(): pl.pallas_call(join_kernel, out_shape=jax.ShapeDtypeStruct((2 * keys.shap...  0.89 us
  transfers between devices with their start and end apart: 7, of which 4 were waited for; matrix products, arithmetic and copies ran while one was open for 0% of the time, Pallas kernels for 37%

profile of v5, /device:TPU:0, one launch (start us, length us, event | category | flops | bytes accessed | tf_op | source)
XLA Modules:
  0.0 42.6 jit_solution(4691700107654745812)
XLA Ops:
  0.6 0.9 %join.1.refs_2_.refs_6_ = bf16[512,128]{1,0:T(8,128)(2,1)S(1)} custom-call(bf16[256,128]{1,0:T(8,128)(2,1)} %keys_ref.1, bf16[256,128]{1,0:T(8,128)(2,1)} %values_ref.1), custom_call_target="tpu_custom_call" | custom-call | tf_op jit(solution)/shard_map/join/pallas_call | solution.py:262
  1.5 3.1 %collective-permute-start = (bf16[512,128]{1,0:T(8,128)(2,1)S(1)}, bf16[512,128]{1,0:T(8,128)(2,1)S(1)}, u32[]{:S(2)}, u32[]{:S(2)}) collective-permute-start(bf16[512,128]{1,0:T(8,128)(2,1)S(1)} %join.1.refs_2_.refs_6_), channel_id=1, source_target_pairs={{0,8},{4,12},{8,16},{12,20},{16,24},{20,28},{24,0},{28,4},{1,9},{5... | collective-permute-start | bytes 393224 | tf_op jit(solution)/shard_map/ppermute | solution.py:17
  4.6 1.5 %collective-permute-start.1 = (bf16[512,128]{1,0:T(8,128)(2,1)S(1)}, bf16[512,128]{1,0:T(8,128)(2,1)S(1)}, u32[]{:S(2)}, u32[]{:S(2)}) collective-permute-start(bf16[512,128]{1,0:T(8,128)(2,1)S(1)} %join.1.refs_2_.refs_6_), channel_id=1, source_target_pairs={{0,4},{4,8},{8,12},{12,16},{16,20},{20,24},{24,28},{28,0},{1,5},{5... | collective-permute-start | bytes 393224 | tf_op jit(solution)/shard_map/ppermute | solution.py:17
  6.2 2.6 %prepare.1 = (bf16[256,2048]{1,0:T(8,128)(2,1)S(1)}, bf16[256,2048]{1,0:T(8,128)(2,1)S(1)}, bf16[2048,256]{1,0:T(8,128)(2,1)S(1)}, bf16[2048,256]{1,0:T(8,128)(2,1)S(1)}, f32[5,256,256]{2,1,0:T(8,128)S(1)}) custom-call(s32[8]{0:T(128)} %lengths_ref.1, bf16[256,2048]{1,0:T(8,128)(2,1)} %q_in.1, bf16[256,2048]{1,0:T(8,128)(2,1)} %g_in.1), custom_call_target="tpu_custom_call" | custom-call | tf_op jit(solution)/shard_map/prepare/pallas_call | solution.py:275
  8.7 1.4 %collective-permute-done.refs_4_.refs_7_ = bf16[512,128]{1,0:T(8,128)(2,1)S(1)} collective-permute-done((bf16[512,128]{1,0:T(8,128)(2,1)S(1)}, bf16[512,128]{1,0:T(8,128)(2,1)S(1)}, u32[]{:S(2)}, u32[]{:S(2)}) %collective-permute-start) | collective-permute-done | bytes 131104 | tf_op jit(solution)/shard_map/ppermute | solution.py:17
  10.2 0.2 collective-permute-start.3
  10.4 2.4 %collective-permute-start.2 = (bf16[512,128]{1,0:T(8,128)(2,1)S(1)}, bf16[512,128]{1,0:T(8,128)(2,1)S(1)}, u32[]{:S(2)}, u32[]{:S(2)}) collective-permute-start(bf16[512,128]{1,0:T(8,128)(2,1)S(1)} %collective-permute-done.refs_4_.refs_7_), channel_id=1, source_target_pairs={{0,4},{4,8},{8,12},{12,16},{16,20},{20,24},{24,28},{28,0},{1,5},{5... | collective-permute-start | bytes 393224 | tf_op jit(solution)/shard_map/ppermute | solution.py:17
  12.7 1.2 %collective-permute-done.1.refs_3_.refs_6_ = bf16[512,128]{1,0:T(8,128)(2,1)S(1)} collective-permute-done((bf16[512,128]{1,0:T(8,128)(2,1)S(1)}, bf16[512,128]{1,0:T(8,128)(2,1)S(1)}, u32[]{:S(2)}, u32[]{:S(2)}) %collective-permute-start.1) | collective-permute-done | bytes 131104 | tf_op jit(solution)/shard_map/ppermute | solution.py:17
  13.9 5.0 %forward_near.1 = (bf16[3,4096,256]{2,1,0:T(8,128)(2,1)S(1)}, f32[4096,256]{1,0:T(8,128)S(1)}, f32[4096,128]{1,0:T(8,128)S(1)}) custom-call(f32[5,256,256]{2,1,0:T(8,128)S(1)} %get-tuple-element.26.refs_0_, bf16[256,2048]{1,0:T(8,128)(2,1)S(1)} %get-tuple-element.27.refs_1_, bf16[512,128]{1,0:T(8,128)(2,1)S(1)} %join.1.refs_2_.refs_6_, ...), custom_call_target="tpu_custom_call" | custom-call | tf_op jit(solution)/shard_map/forward_near/pallas_call | solution.py:310
  19.0 0.0 collective-permute-done.3.refs_8_.refs_10_
  19.0 1.4 %collective-permute-done.2.refs_7_.refs_9_ = bf16[512,128]{1,0:T(8,128)(2,1)S(1)} collective-permute-done((bf16[512,128]{1,0:T(8,128)(2,1)S(1)}, bf16[512,128]{1,0:T(8,128)(2,1)S(1)}, u32[]{:S(2)}, u32[]{:S(2)}) %collective-permute-start.2) | collective-permute-done | bytes 131104 | tf_op jit(solution)/shard_map/ppermute | solution.py:17
  20.4 6.5 %forward_far.1 = (bf16[256,2048]{1,0:T(8,128)(2,1)}, bf16[2,4096,256]{2,1,0:T(8,128)(2,1)S(1)}, bf16[2,256,256]{2,1,0:T(8,128)(2,1)S(1)}, f32[4096,128]{1,0:T(8,128)S(1)}, f32[4096,128]{1,0:T(8,128)S(1)}) custom-call(f32[5,256,256]{2,1,0:T(8,128)S(1)} %get-tuple-element.26.refs_0_, bf16[256,2048]{1,0:T(8,128)(2,1)S(1)} %get-tuple-element.27.refs_1_, ...), custom_call_target="tpu_custom_call" | custom-call | tf_op jit(solution)/shard_map/forward_far/pallas_call | solution.py:330
  26.8 1.7 %collective-permute-start.4 = (bf16[2,256,256]{2,1,0:T(8,128)(2,1)S(1)}, bf16[2,256,256]{2,1,0:T(8,128)(2,1)S(1)}, u32[]{:S(2)}, u32[]{:S(2)}) collective-permute-start(bf16[2,256,256]{2,1,0:T(8,128)(2,1)S(1)} %get-tuple-element.43), channel_id=1, source_target_pairs={{0,24},{4,28},{8,0},{12,4},{16,8},{20,12},{24,16},{28,20},{1,25},{... | collective-permute-start | bytes 786440 | tf_op jit(solution)/shard_map/ppermute | solution.py:17
  28.5 5.2 %backward_near.1 = (f32[256,2048]{1,0:T(8,128)S(1)}, f32[2,256,256]{2,1,0:T(8,128)S(1)}) custom-call(bf16[2048,256]{1,0:T(8,128)(2,1)S(1)} %get-tuple-element.28.refs_2_.refs_0_, bf16[256,2048]{1,0:T(8,128)(2,1)S(1)} %get-tuple-element.29.refs_3_.refs_1_, bf16[2048,256]{1,0:T(8,128)(2,1)S(1)} %get-tuple-element.30.refs_4_.refs_2_, ...), custom_call_target="tpu_custom_call" | custom-call | tf_op jit(solution)/shard_map/backward_near/pallas_call | solution.py:355
  33.8 0.0 collective-permute-done.4
  33.8 0.1 add_convert_fusion
  33.9 3.0 %collective-permute-start.6 = (bf16[256,256]{1,0:T(8,128)(2,1)S(1)}, bf16[256,256]{1,0:T(8,128)(2,1)S(1)}, u32[]{:S(2)}, u32[]{:S(2)}) collective-permute-start(bf16[256,256]{1,0:T(8,128)(2,1)S(1)} %get-tuple-element.46), channel_id=1, source_target_pairs={{0,24},{4,28},{8,0},{12,4},{16,8},{20,12},{24,16},{28,20},{1,25},{... | collective-permute-start | bytes 393224 | tf_op jit(solution)/shard_map/ppermute | solution.py:17
  36.9 0.0 collective-permute-start.5
  36.9 3.0 %backward_last.1 = (bf16[256,2048]{1,0:T(8,128)(2,1)}, f32[1,256,256]{2,1,0:T(8,128)S(1)}) custom-call(bf16[2048,256]{1,0:T(8,128)(2,1)S(1)} %get-tuple-element.28.refs_2_.refs_0_, bf16[256,2048]{1,0:T(8,128)(2,1)S(1)} %get-tuple-element.29.refs_3_.refs_1_, bf16[2048,256]{1,0:T(8,128)(2,1)S(1)} %get-tuple-element.30.refs_4_.refs_2_, ...), custom_call_target="tpu_custom_call" | custom-call | tf_op jit(solution)/shard_map/backward_last/pallas_call | solution.py:355
  39.9 0.0 collective-permute-done.6.refs_1_
  39.9 1.9 %collective-permute-done.5.refs_0_ = bf16[256,256]{1,0:T(8,128)(2,1)S(1)} collective-permute-done((bf16[256,256]{1,0:T(8,128)(2,1)S(1)}, bf16[256,256]{1,0:T(8,128)(2,1)S(1)}, u32[]{:S(2)}, u32[]{:S(2)}) %collective-permute-start.5) | collective-permute-done | bytes 131104 | tf_op jit(solution)/shard_map/ppermute | solution.py:17
  41.8 0.8 %finish.1 = (bf16[256,128]{1,0:T(8,128)(2,1)}, bf16[256,128]{1,0:T(8,128)(2,1)}) custom-call(f32[1,256,256]{2,1,0:T(8,128)S(1)} %get-tuple-element.41.own_ref, bf16[256,256]{1,0:T(8,128)(2,1)S(1)} %collective-permute-done.5.refs_0_, bf16[256,256]{1,0:T(8,128)(2,1)S(1)} %collective-permute-done.6.refs_1_), custom_call_target="tpu_custom_call" | custom-call | tf_op jit(solution)/shard_map/finish/pallas_call | solution.py:295
  (1 shorter events, 0.0 us)
Async XLA Ops:
  1.5 8.6 %collective-permute-start = (bf16[512,128]{1,0:T(8,128)(2,1)S(1)}, bf16[512,128]{1,0:T(8,128)(2,1)S(1)}, u32[]{:S(2)}, u32[]{:S(2)}) collective-permute-start(bf16[512,128]{1,0:T(8,128)(2,1)S(1)} %join.1.refs_2_.refs_6_), channel_id=1, source_target_pairs={{0,8},{4,12},{8,16},{12,20},{16,24},{20,28},{24,0},{28,4},{1,9},{5... | collective-permute-start | bytes 393224 | tf_op jit(solution)/shard_map/ppermute | solution.py:17
  4.6 9.3 %collective-permute-start.1 = (bf16[512,128]{1,0:T(8,128)(2,1)S(1)}, bf16[512,128]{1,0:T(8,128)(2,1)S(1)}, u32[]{:S(2)}, u32[]{:S(2)}) collective-permute-start(bf16[512,128]{1,0:T(8,128)(2,1)S(1)} %join.1.refs_2_.refs_6_), channel_id=1, source_target_pairs={{0,4},{4,8},{8,12},{12,16},{16,20},{20,24},{24,28},{28,0},{1,5},{5... | collective-permute-start | bytes 393224 | tf_op jit(solution)/shard_map/ppermute | solution.py:17
  10.2 8.8 %collective-permute-start.3 = (bf16[512,128]{1,0:T(8,128)(2,1)S(1)}, bf16[512,128]{1,0:T(8,128)(2,1)S(1)}, u32[]{:S(2)}, u32[]{:S(2)}) collective-permute-start(bf16[512,128]{1,0:T(8,128)(2,1)S(1)} %collective-permute-done.refs_4_.refs_7_), channel_id=1, source_target_pairs={{0,8},{4,12},{8,16},{12,20},{16,24},{20,28},{24,0},{28,4},{1,9},{5... | collective-permute-start | bytes 393224 | tf_op jit(solution)/shard_map/ppermute | solution.py:17
  10.4 10.0 %collective-permute-start.2 = (bf16[512,128]{1,0:T(8,128)(2,1)S(1)}, bf16[512,128]{1,0:T(8,128)(2,1)S(1)}, u32[]{:S(2)}, u32[]{:S(2)}) collective-permute-start(bf16[512,128]{1,0:T(8,128)(2,1)S(1)} %collective-permute-done.refs_4_.refs_7_), channel_id=1, source_target_pairs={{0,4},{4,8},{8,12},{12,16},{16,20},{20,24},{24,28},{28,0},{1,5},{5... | collective-permute-start | bytes 393224 | tf_op jit(solution)/shard_map/ppermute | solution.py:17
  26.8 6.9 %collective-permute-start.4 = (bf16[2,256,256]{2,1,0:T(8,128)(2,1)S(1)}, bf16[2,256,256]{2,1,0:T(8,128)(2,1)S(1)}, u32[]{:S(2)}, u32[]{:S(2)}) collective-permute-start(bf16[2,256,256]{2,1,0:T(8,128)(2,1)S(1)} %get-tuple-element.43), channel_id=1, source_target_pairs={{0,24},{4,28},{8,0},{12,4},{16,8},{20,12},{24,16},{28,20},{1,25},{... | collective-permute-start | bytes 786440 | tf_op jit(solution)/shard_map/ppermute | solution.py:17
  33.9 6.0 %collective-permute-start.6 = (bf16[256,256]{1,0:T(8,128)(2,1)S(1)}, bf16[256,256]{1,0:T(8,128)(2,1)S(1)}, u32[]{:S(2)}, u32[]{:S(2)}) collective-permute-start(bf16[256,256]{1,0:T(8,128)(2,1)S(1)} %get-tuple-element.46), channel_id=1, source_target_pairs={{0,24},{4,28},{8,0},{12,4},{16,8},{20,12},{24,16},{28,20},{1,25},{... | collective-permute-start | bytes 393224 | tf_op jit(solution)/shard_map/ppermute | solution.py:17
  36.9 5.0 %collective-permute-start.5 = (bf16[256,256]{1,0:T(8,128)(2,1)S(1)}, bf16[256,256]{1,0:T(8,128)(2,1)S(1)}, u32[]{:S(2)}, u32[]{:S(2)}) collective-permute-start(bf16[256,256]{1,0:T(8,128)(2,1)S(1)} %get-tuple-element.47), channel_id=1, source_target_pairs={{0,28},{4,0},{8,4},{12,8},{16,12},{20,16},{24,20},{28,24},{1,29},{... | collective-permute-start | bytes 393224 | tf_op jit(solution)/shard_map/ppermute | solution.py:17

commit v6 on v5

--- a/solution.py
+++ b/solution.py
@@ -120,8 +120,8 @@
 def finish_kernel(score_scale, own_ref, *refs):
     part_refs, (keys_ref, values_ref) = refs[:-2], refs[-2:]
     width = keys_ref.shape[1]
-    total = own_ref[0]
-    for part_ref in part_refs:
+    total = own_ref[0] + pick_back(part_refs[0][...], part_refs[1][...], 2)
+    for part_ref in part_refs[2:]:
         total = total + part_ref[...].astype(jnp.float32)
     keys_ref[...] = (score_scale * total[:width]).T.astype(jnp.bfloat16)
     values_ref[...] = total[width:].T.astype(jnp.bfloat16)
@@ -365,6 +365,69 @@
     )(qt, g, gt, rate, delta, kept, *kvs, carried, *more)
 
 
+def swap_partners(count, steps, offset):
+    partners = []
+    for i in range(count):
+        j = i + steps if (i // steps) % 2 == offset else i - steps
+        partners.append((i, j if 0 <= j < count else i ^ 1))
+    return partners
+
+
+def swap_back(value, steps):
+    count = lax.axis_size("seq")
+    return [lax.ppermute(value, "seq", swap_partners(count, steps, offset)) for offset in range(2)]
+
+
+def pick_back(first, second, steps):
+    rank, count = lax.axis_index("seq"), lax.axis_size("seq")
+    odd = jnp.full(first.shape, (rank // steps) % 2, jnp.int32) == 1
+    inside = jnp.full(first.shape, rank + steps, jnp.int32) < count
+    moved = jnp.where(odd, second, first).astype(jnp.float32)
+    return jnp.where(inside, moved, 0.0)
+
+
+def merge_kernel(steps, near_ref, first_ref, second_ref, *out_refs):
+    for slot, out_ref in enumerate(out_refs):
+        moved = pick_back(first_ref[slot], second_ref[slot], steps)
+        out_ref[...] = (near_ref[slot].astype(jnp.float32) + moved).astype(jnp.bfloat16)
+
+
+def merge_call(near_grads, moved, steps):
+    slots, *shape = near_grads.shape
+    return pl.pallas_call(
+        functools.partial(merge_kernel, steps),
+        out_shape=(jax.ShapeDtypeStruct(shape, jnp.bfloat16),) * slots,
+        in_specs=[VMEM] * 3,
+        out_specs=(VMEM,) * slots,
+        compiler_params=pltpu.CompilerParams(vmem_limit_bytes=1 << 20),
+        name="merge",
+    )(near_grads, *moved)
+
+
+def choose_kernel(steps, first_ref, second_ref, out_ref):
+    odd = (lax.axis_index("seq") // steps) % 2 == 1
+
+    @pl.when(odd)
+    def _():
+        out_ref[...] = first_ref[...]
+
+    @pl.when(jnp.logical_not(odd))
+    def _():
+        out_ref[...] = second_ref[...]
+
+
+def swap_forward(value, steps):
+    moved = swap_back(value, steps)
+    return pl.pallas_call(
+        functools.partial(choose_kernel, steps),
+        out_shape=jax.ShapeDtypeStruct(value.shape, value.dtype),
+        in_specs=[VMEM] * 2,
+        out_specs=VMEM,
+        compiler_params=pltpu.CompilerParams(vmem_limit_bytes=1 << 20),
+        name="choose",
+    )(*moved)
+
+
 def shards(queries, keys, values, lengths, grad_out):
     width = keys.shape[1]
     head_count = queries.shape[1] // width
@@ -377,7 +440,7 @@
 
     near = reach // 2 + 1
     own = join_call(keys, values)
-    two = ring_shift(own, 2)
+    two = swap_forward(own, 2)
     one = ring_shift(own, 1)
     queries, grad_out, queries_t, grads_t, bias = prepare_call(
         lengths, queries, grad_out, reach + 1
@@ -395,17 +458,17 @@
     out, far_steps, far_grads, rate, delta = far_call(
         bias, queries, queries_t, grad_out, grads_t, total, top, window[near:], near, pack_f, head_count, score_scale
     )
-    moved = ring_shift(far_grads, -(reach // 2))
+    moved = swap_back(far_grads, reach // 2)
     shared = (queries_t, grad_out, grads_t, rate, delta, kept)
     dq, near_grads = later_call(
         *shared, window[1:near], far_steps, window[near:], 1, pack_2, head_count, score_scale
     )
-    near_grads = (near_grads + moved.astype(jnp.float32)).astype(jnp.bfloat16)
-    while near_grads.shape[0] > 2:
-        half = near_grads.shape[0] // 2
-        back = ring_shift(near_grads[half:], -half)
-        near_grads = (near_grads[:half].astype(jnp.float32) + back.astype(jnp.float32)).astype(jnp.bfloat16)
-    received = [ring_shift(near_grads[i], -1 - i) for i in range(near_grads.shape[0])]
+    parts = merge_call(near_grads, moved, reach // 2)
+    while len(parts) > 2:
+        half = len(parts) // 2
+        moved = swap_back(jnp.stack(parts[half:]), half)
+        parts = merge_call(jnp.stack(parts[:half]), moved, half)
+    received = [*swap_back(parts[1], 2), ring_shift(parts[0], -1)]
     dq, own_grads = later_call(
         *shared, window[:1], dq, [], 0, pack_3, head_count, score_scale
     )

time: 42.8 us -> 42.1 us (0.984)
  waiting for transfers between devices: 5.94 us -> 1.62 us
  starting transfers between devices: 11.9 us -> 15.5 us
    ppermute x0 -> x6, starting transfers between devices: none -> 7.37 us  [swap_back(): lax.ppermute(value, 'seq', swap_partners(count, steps, offset))]
    ppermute x7 -> x4, waiting for transfers between devices: 5.94 us -> 0.68 us  [ring_shift(): lax.ppermute(value, 'seq', [(i, (i + steps) % count) for i in range(count)])]
    ppermute x7 -> x4, starting transfers between devices: 11.9 us -> 8.13 us  [ring_shift(): lax.ppermute(value, 'seq', [(i, (i + steps) % count) for i in range(count)])]
    ppermute x0 -> x6, waiting for transfers between devices: none -> 0.94 us  [swap_back(): lax.ppermute(value, 'seq', swap_partners(count, steps, offset))]
  transfers between devices with their start and end apart: 7 -> 10, of which waited for: 4 -> 5; matrix products, arithmetic and copies ran while one was open for 0% -> 0% of each run, Pallas kernels for 37% -> 38%
where the time goes in v6:
time: 42.1 us; the launch traced here: 41.9 us
  Pallas kernels  24.1 us (57%)
  starting transfers between devices  15.5 us (37%)
  waiting for transfers between devices  1.62 us (4%)
  between operations  0.72 us (2%)
    pallas_call x2, Pallas kernels, later_call(): pl.pallas_call(functools.partial(later_kernel, first_slot, slots, pack, h...  8.23 us
    ppermute x4, starting transfers between devices, ring_shift(): lax.ppermute(value, 'seq', [(i, (i + steps) % count) for i in range(count)])  8.13 us
    ppermute x6, starting transfers between devices, swap_back(): lax.ppermute(value, 'seq', swap_partners(count, steps, offset))  7.37 us
    pallas_call x1, Pallas kernels, far_call(): pl.pallas_call(functools.partial(far_kernel, first_slot, slots, pack, hea...  6.45 us
    pallas_call x1, Pallas kernels, near_call(): pl.pallas_call(functools.partial(near_kernel, slots, pack, head_count, sc...  5.03 us
    pallas_call x1, Pallas kernels, prepare_call(): pl.pallas_call(functools.partial(prepare_kernel, slot_count), out_shape=(...  2.56 us
    ppermute x6, waiting for transfers between devices, swap_back(): lax.ppermute(value, 'seq', swap_partners(count, steps, offset))  0.94 us
    pallas_call x1, Pallas kernels, join_call(): pl.pallas_call(join_kernel, out_shape=jax.ShapeDtypeStruct((2 * keys.shap...  0.89 us
  transfers between devices with their start and end apart: 10, of which 5 were waited for; matrix products, arithmetic and copies ran while one was open for 0% of the time, Pallas kernels for 38%

profile of v6, /device:TPU:0, one launch (start us, length us, event | category | flops | bytes accessed | tf_op | source)
XLA Modules:
  0.0 41.9 jit_solution(13340007440982136268)
XLA Ops:
  0.6 0.9 %join.1.refs_2_.refs_6_ = bf16[512,128]{1,0:T(8,128)(2,1)S(1)} custom-call(bf16[256,128]{1,0:T(8,128)(2,1)} %keys_ref.1, bf16[256,128]{1,0:T(8,128)(2,1)} %values_ref.1), custom_call_target="tpu_custom_call" | custom-call | tf_op jit(solution)/shard_map/join/pallas_call | solution.py:262
  1.5 3.1 %collective-permute-start.1 = (bf16[512,128]{1,0:T(8,128)(2,1)S(1)}, bf16[512,128]{1,0:T(8,128)(2,1)S(1)}, u32[]{:S(2)}, u32[]{:S(2)}) collective-permute-start(bf16[512,128]{1,0:T(8,128)(2,1)S(1)} %join.1.refs_2_.refs_6_), channel_id=1, source_target_pairs={{0,4},{4,0},{8,16},{12,20},{16,8},{20,12},{24,28},{28,24},{1,5},{5... | collective-permute-start | bytes 393224 | tf_op jit(solution)/shard_map/ppermute | solution.py:378
  4.6 1.6 %collective-permute-start = (bf16[512,128]{1,0:T(8,128)(2,1)S(1)}, bf16[512,128]{1,0:T(8,128)(2,1)S(1)}, u32[]{:S(2)}, u32[]{:S(2)}) collective-permute-start(bf16[512,128]{1,0:T(8,128)(2,1)S(1)} %join.1.refs_2_.refs_6_), channel_id=1, source_target_pairs={{0,8},{4,12},{8,0},{12,4},{16,24},{20,28},{24,16},{28,20},{1,9},{5... | collective-permute-start | bytes 393224 | tf_op jit(solution)/shard_map/ppermute | solution.py:378
  6.2 1.5 %collective-permute-start.2 = (bf16[512,128]{1,0:T(8,128)(2,1)S(1)}, bf16[512,128]{1,0:T(8,128)(2,1)S(1)}, u32[]{:S(2)}, u32[]{:S(2)}) collective-permute-start(bf16[512,128]{1,0:T(8,128)(2,1)S(1)} %join.1.refs_2_.refs_6_), channel_id=1, source_target_pairs={{0,4},{4,8},{8,12},{12,16},{16,20},{20,24},{24,28},{28,0},{1,5},{5... | collective-permute-start | bytes 393224 | tf_op jit(solution)/shard_map/ppermute | solution.py:17
  7.7 2.6 %prepare.1 = (bf16[256,2048]{1,0:T(8,128)(2,1)S(1)}, bf16[256,2048]{1,0:T(8,128)(2,1)S(1)}, bf16[2048,256]{1,0:T(8,128)(2,1)S(1)}, bf16[2048,256]{1,0:T(8,128)(2,1)S(1)}, f32[5,256,256]{2,1,0:T(8,128)S(1)}) custom-call(s32[8]{0:T(128)} %lengths_ref.1, bf16[256,2048]{1,0:T(8,128)(2,1)} %q_in.1, bf16[256,2048]{1,0:T(8,128)(2,1)} %g_in.1), custom_call_target="tpu_custom_call" | custom-call | tf_op jit(solution)/shard_map/prepare/pallas_call | solution.py:275
  10.3 0.0 collective-permute-done.1.second_ref
  10.3 0.0 collective-permute-done.first_ref
  10.4 0.9 %collective-permute-start.4 = (bf16[512,128]{1,0:T(8,128)(2,1)S(1)}, bf16[512,128]{1,0:T(8,128)(2,1)S(1)}, u32[]{:S(2)}, u32[]{:S(2)}) collective-permute-start(bf16[512,128]{1,0:T(8,128)(2,1)S(1)} %choose.1.refs_4_.refs_7_), channel_id=1, source_target_pairs={{0,8},{4,12},{8,16},{12,20},{16,24},{20,28},{24,0},{28,4},{1,9},{5... | collective-permute-start | bytes 393224 | tf_op jit(solution)/shard_map/ppermute | solution.py:17
  11.3 2.9 %collective-permute-start.3 = (bf16[512,128]{1,0:T(8,128)(2,1)S(1)}, bf16[512,128]{1,0:T(8,128)(2,1)S(1)}, u32[]{:S(2)}, u32[]{:S(2)}) collective-permute-start(bf16[512,128]{1,0:T(8,128)(2,1)S(1)} %choose.1.refs_4_.refs_7_), channel_id=1, source_target_pairs={{0,4},{4,8},{8,12},{12,16},{16,20},{20,24},{24,28},{28,0},{1,5},{5... | collective-permute-start | bytes 393224 | tf_op jit(solution)/shard_map/ppermute | solution.py:17
  14.2 0.5 %collective-permute-done.2.refs_3_.refs_6_ = bf16[512,128]{1,0:T(8,128)(2,1)S(1)} collective-permute-done((bf16[512,128]{1,0:T(8,128)(2,1)S(1)}, bf16[512,128]{1,0:T(8,128)(2,1)S(1)}, u32[]{:S(2)}, u32[]{:S(2)}) %collective-permute-start.2) | collective-permute-done | bytes 131104 | tf_op jit(solution)/shard_map/ppermute | solution.py:17
  14.7 5.0 %forward_near.1 = (bf16[3,4096,256]{2,1,0:T(8,128)(2,1)S(1)}, f32[4096,256]{1,0:T(8,128)S(1)}, f32[4096,128]{1,0:T(8,128)S(1)}) custom-call(f32[5,256,256]{2,1,0:T(8,128)S(1)} %get-tuple-element.28.refs_0_, bf16[256,2048]{1,0:T(8,128)(2,1)S(1)} %get-tuple-element.29.refs_1_, bf16[512,128]{1,0:T(8,128)(2,1)S(1)} %join.1.refs_2_.refs_6_, ...), custom_call_target="tpu_custom_call" | custom-call | tf_op jit(solution)/shard_map/forward_near/pallas_call | solution.py:310
  19.8 0.1 collective-permute-done.3.refs_7_.refs_9_
  19.9 6.5 %forward_far.1 = (bf16[256,2048]{1,0:T(8,128)(2,1)}, bf16[2,4096,256]{2,1,0:T(8,128)(2,1)S(1)}, bf16[2,256,256]{2,1,0:T(8,128)(2,1)S(1)}, f32[4096,128]{1,0:T(8,128)S(1)}, f32[4096,128]{1,0:T(8,128)S(1)}) custom-call(f32[5,256,256]{2,1,0:T(8,128)S(1)} %get-tuple-element.28.refs_0_, bf16[256,2048]{1,0:T(8,128)(2,1)S(1)} %get-tuple-element.29.refs_1_, ...), custom_call_target="tpu_custom_call" | custom-call | tf_op jit(solution)/shard_map/forward_far/pallas_call | solution.py:330
  26.4 0.1 collective-permute-start.6
  26.4 1.4 %collective-permute-start.5 = (bf16[2,256,256]{2,1,0:T(8,128)(2,1)S(1)}, bf16[2,256,256]{2,1,0:T(8,128)(2,1)S(1)}, u32[]{:S(2)}, u32[]{:S(2)}) collective-permute-start(bf16[2,256,256]{2,1,0:T(8,128)(2,1)S(1)} %get-tuple-element.45), channel_id=1, source_target_pairs={{0,8},{4,12},{8,0},{12,4},{16,24},{20,28},{24,16},{28,20},{1,9},{5... | collective-permute-start | bytes 786440 | tf_op jit(solution)/shard_map/ppermute | solution.py:378
  27.8 5.2 %backward_near.1 = (f32[256,2048]{1,0:T(8,128)S(1)}, f32[2,256,256]{2,1,0:T(8,128)S(1)}) custom-call(bf16[2048,256]{1,0:T(8,128)(2,1)S(1)} %get-tuple-element.30.refs_2_.refs_0_, bf16[256,2048]{1,0:T(8,128)(2,1)S(1)} %get-tuple-element.31.refs_3_.refs_1_, bf16[2048,256]{1,0:T(8,128)(2,1)S(1)} %get-tuple-element.32.refs_4_.refs_2_, ...), custom_call_target="tpu_custom_call" | custom-call | tf_op jit(solution)/shard_map/backward_near/pallas_call | solution.py:355
  33.1 0.1 collective-permute-done.6.second_ref
  33.2 0.1 collective-permute-done.5.first_ref
  33.2 0.1 merge.1
  33.3 2.8 %collective-permute-start.9 = (bf16[256,256]{1,0:T(8,128)(2,1)S(1)}, bf16[256,256]{1,0:T(8,128)(2,1)S(1)}, u32[]{:S(2)}, u32[]{:S(2)}) collective-permute-start(bf16[256,256]{1,0:T(8,128)(2,1)S(1)} %get-tuple-element.47), channel_id=1, source_target_pairs={{0,28},{4,0},{8,4},{12,8},{16,12},{20,16},{24,20},{28,24},{1,29},{... | collective-permute-start | bytes 393224 | tf_op jit(solution)/shard_map/ppermute | solution.py:17
  36.1 1.2 %collective-permute-start.7 = (bf16[256,256]{1,0:T(8,128)(2,1)S(1)}, bf16[256,256]{1,0:T(8,128)(2,1)S(1)}, u32[]{:S(2)}, u32[]{:S(2)}) collective-permute-start(bf16[256,256]{1,0:T(8,128)(2,1)S(1)} %get-tuple-element.46), channel_id=1, source_target_pairs={{0,8},{4,12},{8,0},{12,4},{16,24},{20,28},{24,16},{28,20},{1,9},{5... | collective-permute-start | bytes 393224 | tf_op jit(solution)/shard_map/ppermute | solution.py:378
  37.3 3.0 %backward_last.1 = (bf16[256,2048]{1,0:T(8,128)(2,1)}, f32[1,256,256]{2,1,0:T(8,128)S(1)}) custom-call(bf16[2048,256]{1,0:T(8,128)(2,1)S(1)} %get-tuple-element.30.refs_2_.refs_0_, bf16[256,2048]{1,0:T(8,128)(2,1)S(1)} %get-tuple-element.31.refs_3_.refs_1_, bf16[2048,256]{1,0:T(8,128)(2,1)S(1)} %get-tuple-element.32.refs_4_.refs_2_, ...), custom_call_target="tpu_custom_call" | custom-call | tf_op jit(solution)/shard_map/backward_last/pallas_call | solution.py:355
  40.3 0.8 %collective-permute-done.8.refs_1_ = bf16[256,256]{1,0:T(8,128)(2,1)S(1)} collective-permute-done((bf16[256,256]{1,0:T(8,128)(2,1)S(1)}, bf16[256,256]{1,0:T(8,128)(2,1)S(1)}, u32[]{:S(2)}, u32[]{:S(2)}) %collective-permute-start.8) | collective-permute-done | bytes 131104 | tf_op jit(solution)/shard_map/ppermute | solution.py:378
  41.1 0.8 %finish.1 = (bf16[256,128]{1,0:T(8,128)(2,1)}, bf16[256,128]{1,0:T(8,128)(2,1)}) custom-call(f32[1,256,256]{2,1,0:T(8,128)S(1)} %get-tuple-element.43.own_ref, bf16[256,256]{1,0:T(8,128)(2,1)S(1)} %collective-permute-done.7.refs_0_, bf16[256,256]{1,0:T(8,128)(2,1)S(1)} %collective-permute-done.8.refs_1_, bf16[256,256]{1,0:T(8,128)(2,1)S(1)} %collective-permute-done.9.refs_2_), custom_call_target="tpu_custom_call" | custom-call | tf_op jit(solution)/shard_map/finish/pallas_call | solution.py:295
  (5 shorter events, 0.0 us)
Async XLA Ops:
  1.5 8.8 %collective-permute-start.1 = (bf16[512,128]{1,0:T(8,128)(2,1)S(1)}, bf16[512,128]{1,0:T(8,128)(2,1)S(1)}, u32[]{:S(2)}, u32[]{:S(2)}) collective-permute-start(bf16[512,128]{1,0:T(8,128)(2,1)S(1)} %join.1.refs_2_.refs_6_), channel_id=1, source_target_pairs={{0,4},{4,0},{8,16},{12,20},{16,8},{20,12},{24,28},{28,24},{1,5},{5... | collective-permute-start | bytes 393224 | tf_op jit(solution)/shard_map/ppermute | solution.py:378
  4.6 5.7 %collective-permute-start = (bf16[512,128]{1,0:T(8,128)(2,1)S(1)}, bf16[512,128]{1,0:T(8,128)(2,1)S(1)}, u32[]{:S(2)}, u32[]{:S(2)}) collective-permute-start(bf16[512,128]{1,0:T(8,128)(2,1)S(1)} %join.1.refs_2_.refs_6_), channel_id=1, source_target_pairs={{0,8},{4,12},{8,0},{12,4},{16,24},{20,28},{24,16},{28,20},{1,9},{5... | collective-permute-start | bytes 393224 | tf_op jit(solution)/shard_map/ppermute | solution.py:378
  6.2 8.5 %collective-permute-start.2 = (bf16[512,128]{1,0:T(8,128)(2,1)S(1)}, bf16[512,128]{1,0:T(8,128)(2,1)S(1)}, u32[]{:S(2)}, u32[]{:S(2)}) collective-permute-start(bf16[512,128]{1,0:T(8,128)(2,1)S(1)} %join.1.refs_2_.refs_6_), channel_id=1, source_target_pairs={{0,4},{4,8},{8,12},{12,16},{16,20},{20,24},{24,28},{28,0},{1,5},{5... | collective-permute-start | bytes 393224 | tf_op jit(solution)/shard_map/ppermute | solution.py:17
  10.4 9.4 %collective-permute-start.4 = (bf16[512,128]{1,0:T(8,128)(2,1)S(1)}, bf16[512,128]{1,0:T(8,128)(2,1)S(1)}, u32[]{:S(2)}, u32[]{:S(2)}) collective-permute-start(bf16[512,128]{1,0:T(8,128)(2,1)S(1)} %choose.1.refs_4_.refs_7_), channel_id=1, source_target_pairs={{0,8},{4,12},{8,16},{12,20},{16,24},{20,28},{24,0},{28,4},{1,9},{5... | collective-permute-start | bytes 393224 | tf_op jit(solution)/shard_map/ppermute | solution.py:17
  11.3 8.6 %collective-permute-start.3 = (bf16[512,128]{1,0:T(8,128)(2,1)S(1)}, bf16[512,128]{1,0:T(8,128)(2,1)S(1)}, u32[]{:S(2)}, u32[]{:S(2)}) collective-permute-start(bf16[512,128]{1,0:T(8,128)(2,1)S(1)} %choose.1.refs_4_.refs_7_), channel_id=1, source_target_pairs={{0,4},{4,8},{8,12},{12,16},{16,20},{20,24},{24,28},{28,0},{1,5},{5... | collective-permute-start | bytes 393224 | tf_op jit(solution)/shard_map/ppermute | solution.py:17
  26.4 6.8 %collective-permute-start.6 = (bf16[2,256,256]{2,1,0:T(8,128)(2,1)S(1)}, bf16[2,256,256]{2,1,0:T(8,128)(2,1)S(1)}, u32[]{:S(2)}, u32[]{:S(2)}) collective-permute-start(bf16[2,256,256]{2,1,0:T(8,128)(2,1)S(1)} %get-tuple-element.45), channel_id=1, source_target_pairs={{0,4},{4,0},{8,16},{12,20},{16,8},{20,12},{24,28},{28,24},{1,5},{5... | collective-permute-start | bytes 786440 | tf_op jit(solution)/shard_map/ppermute | solution.py:378
  26.4 6.8 %collective-permute-start.5 = (bf16[2,256,256]{2,1,0:T(8,128)(2,1)S(1)}, bf16[2,256,256]{2,1,0:T(8,128)(2,1)S(1)}, u32[]{:S(2)}, u32[]{:S(2)}) collective-permute-start(bf16[2,256,256]{2,1,0:T(8,128)(2,1)S(1)} %get-tuple-element.45), channel_id=1, source_target_pairs={{0,8},{4,12},{8,0},{12,4},{16,24},{20,28},{24,16},{28,20},{1,9},{5... | collective-permute-start | bytes 786440 | tf_op jit(solution)/shard_map/ppermute | solution.py:378
  33.3 7.0 %collective-permute-start.9 = (bf16[256,256]{1,0:T(8,128)(2,1)S(1)}, bf16[256,256]{1,0:T(8,128)(2,1)S(1)}, u32[]{:S(2)}, u32[]{:S(2)}) collective-permute-start(bf16[256,256]{1,0:T(8,128)(2,1)S(1)} %get-tuple-element.47), channel_id=1, source_target_pairs={{0,28},{4,0},{8,4},{12,8},{16,12},{20,16},{24,20},{28,24},{1,29},{... | collective-permute-start | bytes 393224 | tf_op jit(solution)/shard_map/ppermute | solution.py:17
  36.1 5.0 %collective-permute-start.8 = (bf16[256,256]{1,0:T(8,128)(2,1)S(1)}, bf16[256,256]{1,0:T(8,128)(2,1)S(1)}, u32[]{:S(2)}, u32[]{:S(2)}) collective-permute-start(bf16[256,256]{1,0:T(8,128)(2,1)S(1)} %get-tuple-element.46), channel_id=1, source_target_pairs={{0,4},{4,0},{8,16},{12,20},{16,8},{20,12},{24,28},{28,24},{1,5},{5... | collective-permute-start | bytes 393224 | tf_op jit(solution)/shard_map/ppermute | solution.py:378
  36.1 5.0 %collective-permute-start.7 = (bf16[256,256]{1,0:T(8,128)(2,1)S(1)}, bf16[256,256]{1,0:T(8,128)(2,1)S(1)}, u32[]{:S(2)}, u32[]{:S(2)}) collective-permute-start(bf16[256,256]{1,0:T(8,128)(2,1)S(1)} %get-tuple-element.46), channel_id=1, source_target_pairs={{0,8},{4,12},{8,0},{12,4},{16,24},{20,28},{24,16},{28,20},{1,9},{5... | collective-permute-start | bytes 393224 | tf_op jit(solution)/shard_map/ppermute | solution.py:378
